TPU v7x, 128 devices: a whole 4x4x4 slice. The times are simulated.
128 devices in a mesh: rep: 2 (over core), dp: 64 (over x, y, z).
Axes of the slice: x: 4, y: 4, z: 4, core: 2. Of those that a mesh axis runs over, the one named last changes fastest.
Arguments:
- x: bfloat16 [128, 2048, 1024], P(('rep', 'dp')), parts along dimension 0
- dy: bfloat16 [128, 2048, 1024], P(('rep', 'dp')), parts along dimension 0
- w_gate: bfloat16 [2, 1024, 2816], P(None, 'dp')
- w_up: bfloat16 [2, 1024, 2816], P(None, 'dp')
- w_down: bfloat16 [2, 2816, 1024], P(None, 'dp')
Outputs:
- output 1: bfloat16 [128, 2048, 1024], P(('rep', 'dp')), parts along dimension 0
- output 2: bfloat16 [4, 1024, 2816], P('rep', 'dp'), parts along dimension 0
- output 3: bfloat16 [4, 1024, 2816], P('rep', 'dp'), parts along dimension 0
- output 4: bfloat16 [4, 2816, 1024], P('rep', 'dp'), parts along dimension 0
There are 2 independent parts. A program takes and returns all parts, laid end to end along the dimension named above; an argument that names none is the same for every part.
All inputs are finite; a program needn't handle non-finite values.
Results may differ from a plain program's by a relative error of at most 0.018.
Values are sent between devices in bfloat16 or wider.
A program may use at most 1.5 GiB of HBM per device.

v0:
```python
import jax
import jax.numpy as jnp
from jax import lax

NAMES = ("w_gate", "w_up", "w_down")


def matmul(a, w):
    return jnp.dot(a, w, preferred_element_type=jnp.float32).astype(jnp.bfloat16)


def normed(h):
    wide = h.astype(jnp.float32)
    scale = lax.rsqrt(jnp.mean(wide**2, -1, keepdims=True) + 1e-6)
    return (wide * scale).astype(jnp.bfloat16)


def layer(h, w):
    a = normed(h)
    gate = jnp.dot(a, w["w_gate"], preferred_element_type=jnp.float32)
    up = jnp.dot(a, w["w_up"], preferred_element_type=jnp.float32)
    return h + matmul((jax.nn.silu(gate) * up).astype(jnp.bfloat16), w["w_down"])


def stack(weights, h):
    for number in range(weights["w_gate"].shape[0]):
        h = layer(h, {name: w[number] for name, w in weights.items()})
    return h


def solution(mesh):
    groups = mesh.shape["rep"]

    def step(x, dy, *weights):
        shape = x.shape
        x, dy = (t.reshape(groups, -1, *t.shape[1:]) for t in (x, dy))

        def of_a_group(x, dy):
            _, back = jax.vjp(stack, dict(zip(NAMES, weights, strict=True)), x)
            by_weights, by_x = back(dy)
            return (by_x, *(by_weights[name] for name in NAMES))

        by_x, *by_weights = jax.vmap(of_a_group)(x, dy)
        return (by_x.reshape(shape), *(t.reshape(-1, *t.shape[2:]) for t in by_weights))

    return step
```

profile of v0, /device:TPU:0, one launch (start us, length us, event | category | flops | bytes accessed | tf_op | source)
XLA Modules:
  0.0 2033.2 jit_solution(16854335039091362549)
XLA Ops:
  7.2 1.6 fusion.111
  8.9 1.6 fusion.110
  10.6 2.1 fusion.112
  14.5 3.1 fusion.34
  17.5 6.4 copy.11
  24.6 6.5 copy.10
  31.1 53.2 %all-gather.29.cloned.1.call-done = bf16[1,1024,2816]{2,1,0:T(8,128)(2,1)} async-done(((bf16[1,16,2816]{2,1,0:T(8,128)(2,1)}), bf16[1,1024,2816]{2,1,0:T(8,128)(2,1)}) %all-gather.29.cloned.1.call-update) | async-done | bytes 5767184 | tf_op jit(solution)/vmap(jvp())/squeeze | solution.py:27
  84.3 19.8 fusion.71
  104.1 52.7 %all-gather.31.cloned.1.call-done = bf16[1,1024,2816]{2,1,0:T(8,128)(2,1)} async-done(((bf16[1,16,2816]{2,1,0:T(8,128)(2,1)}), bf16[1,1024,2816]{2,1,0:T(8,128)(2,1)}) %all-gather.31.cloned.1.call-update) | async-done | bytes 5767184 | tf_op jit(solution)/vmap(jvp())/squeeze | solution.py:27
  156.8 19.9 fusion.67
  176.7 19.7 fusion.26
  196.3 50.4 %all-gather.33.cloned.1.call-done = bf16[1,2816,1024]{2,0,1:T(2,128)(2,1)} async-done(((bf16[1,44,1024]{2,0,1:T(2,128)(2,1)}), bf16[1,2816,1024]{2,0,1:T(2,128)(2,1)}) %all-gather.33.cloned.1.call-update) | async-done | bytes 5767184 | tf_op jit(solution)/vmap(jvp())/squeeze | solution.py:27
  246.8 22.8 %fusion.42 = (f32[2048]{0:T(1024)S(1)}, bf16[1,1,2048,1024]{2,3,1,0:T(8,128)(2,1)}) fusion(bf16[2048,2816]{1,0:T(8,128)(2,1)} %fusion.26, bf16[1,2816,1024]{2,0,1:T(2,128)(2,1)} %all-gather.33.cloned.1.call-done, bf16[1,2048,1024]{1,2,0:T(8,128)(2,1)} %copy.11), kind=kOutput, calls=%fused_computation.62 | convolution fusion | flops 11821643776 | bytes 25698304 | tf_op jit(solution)/vmap(jvp())/dot_general | solution.py:9
  270.2 67.2 %all-gather.37.cloned.1.call-done = bf16[1,2816,1024]{2,0,1:T(2,128)(2,1)} async-done(((bf16[1,44,1024]{2,0,1:T(2,128)(2,1)}), bf16[1,2816,1024]{2,0,1:T(2,128)(2,1)}) %all-gather.37.cloned.1.call-update) | async-done | bytes 5767184 | tf_op jit(solution)/vmap(jvp())/squeeze | solution.py:27
  337.4 19.9 convolution_convert_fusion.1
  357.3 53.2 %all-gather.35.cloned.1.call-done = bf16[1,1024,2816]{2,1,0:T(8,128)(2,1)} async-done(((bf16[1,16,2816]{2,1,0:T(8,128)(2,1)}), bf16[1,1024,2816]{2,1,0:T(8,128)(2,1)}) %all-gather.35.cloned.1.call-update) | async-done | bytes 5767184 | tf_op jit(solution)/vmap(jvp())/squeeze | solution.py:27
  410.6 19.9 fusion.64
  430.5 23.8 %fusion.45 = f32[1,1024,2816]{2,1,0:T(8,128)} fusion(bf16[2048,2816]{1,0:T(8,128)(2,1)} %convolution_convert_fusion.1, f32[2048,2816]{1,0:T(8,128)} %fusion.64, bf16[1,1,2048,1024]{2,3,1,0:T(8,128)(2,1)} %get-tuple-element.37, f32[2048]{0:T(1024)S(1)} %bitcast.282), kind=kOutput, calls=%fused_computation.65 | convolution fusion | flops 11852054528 | bytes 50339840 | tf_op jit(solution)/vmap(transpose(jvp()))/dot_general | solution.py:21
  454.4 29.2 %all-gather.39.cloned.1.call-done = bf16[1,1024,2816]{2,1,0:T(8,128)(2,1)} async-done(((bf16[1,16,2816]{2,1,0:T(8,128)(2,1)}), bf16[1,1024,2816]{2,1,0:T(8,128)(2,1)}) %all-gather.39.cloned.1.call-update) | async-done | bytes 5767184 | tf_op jit(solution)/vmap(jvp())/squeeze | solution.py:27
  483.6 19.9 fusion.59
  503.4 23.3 %fusion.6 = bf16[2048,2816]{1,0:T(8,128)(2,1)} fusion(f32[2048,2816]{1,0:T(8,128)} %fusion.64, f32[2048,2816]{1,0:T(8,128)} %fusion.59, bf16[2048,2816]{1,0:T(8,128)(2,1)} %convolution_convert_fusion.1), kind=kLoop, calls=%fused_computation.10 | loop fusion | flops 69206016 | bytes 69206016
  526.7 21.9 %fusion.24 = bf16[2048,1024]{0,1:T(8,128)(2,1)} fusion(bf16[2048,2816]{1,0:T(8,128)(2,1)} %convolution_convert_fusion.1, f32[2048,2816]{1,0:T(8,128)} %fusion.64, bf16[1,1024,2816]{2,1,0:T(8,128)(2,1)} %all-gather.39.cloned.1.call-done), kind=kOutput, calls=%fused_computation.33 | convolution fusion | flops 11845763072 | bytes 44564480 | tf_op jit(solution)/vmap(transpose(jvp()))/dot_general | solution.py:21
  548.6 18.9 fusion.44
  567.6 3.3 fusion.77
  570.9 21.6 %convolution_convert_fusion = bf16[2048,2816]{1,0:T(8,128)(2,1)} fusion(bf16[1,1,2048,1024]{2,3,1,0:T(8,128)(2,1)S(1)} %fusion.77, bf16[1,2816,1024]{2,0,1:T(2,128)(2,1)} %all-gather.33.cloned.1.call-done), kind=kOutput, calls=%fused_computation.48 | convolution fusion | flops 11816927232 | bytes 21495808 | tf_op jit(solution)/vmap(transpose(jvp()))/dot_general | solution.py:9
  592.5 23.3 %fusion.9 = bf16[2048,2816]{1,0:T(8,128)(2,1)} fusion(f32[2048,2816]{1,0:T(8,128)} %fusion.71, f32[2048,2816]{1,0:T(8,128)} %fusion.67, bf16[2048,2816]{1,0:T(8,128)(2,1)} %convolution_convert_fusion), kind=kLoop, calls=%fused_computation.13 | loop fusion | flops 69206016 | bytes 69206016
  615.7 21.4 %fusion.20 = bf16[2048,1024]{0,1:T(8,128)(2,1)} fusion(bf16[2048,2816]{1,0:T(8,128)(2,1)} %convolution_convert_fusion, f32[2048,2816]{1,0:T(8,128)} %fusion.71, bf16[1,1024,2816]{2,1,0:T(8,128)(2,1)} %all-gather.31.cloned.1.call-done), kind=kOutput, calls=%fused_computation.31 | convolution fusion | flops 11845763072 | bytes 44564480 | tf_op jit(solution)/vmap(transpose(jvp()))/dot_general | solution.py:21
  637.2 20.5 %fusion.40 = (f32[2048]{0:T(1024)S(1)}, bf16[2048,1024]{0,1:T(8,128)(2,1)}) fusion(bf16[1,2048,1024]{1,2,0:T(8,128)(2,1)} %copy.11, bf16[2048,1024]{0,1:T(8,128)(2,1)} %fusion.20, bf16[2048,2816]{1,0:T(8,128)(2,1)} %fusion.9, bf16[1,1024,2816]{2,1,0:T(8,128)(2,1)} %all-gather.29.cloned.1.call-done), kind=kOutput, calls=%fused_computation.60 | convolution fusion | flops 11821643776 | bytes 29892608 | tf_op jit(solution)/vmap(transpose(jvp()))/dot_general | solution.py:20
  658.3 23.4 %fusion.48 = f32[1,1024,2816]{2,1,0:T(8,128)} fusion(bf16[2048,2816]{1,0:T(8,128)(2,1)} %convolution_convert_fusion, f32[2048,2816]{1,0:T(8,128)} %fusion.71, bf16[1,2048,1024]{1,2,0:T(8,128)(2,1)} %copy.11, f32[2048]{0:T(1024)S(1)} %bitcast.286), kind=kOutput, calls=%fused_computation.66 | convolution fusion | flops 11852054528 | bytes 50339840 | tf_op jit(solution)/vmap(transpose(jvp()))/dot_general | solution.py:21
  681.7 18.9 convolution_bitcast_fusion.1
  701.3 18.6 convolution_bitcast_fusion.2
  720.0 19.1 convolution_bitcast_fusion
  739.1 24.3 %fusion.51 = f32[1,2816,1024]{2,1,0:T(8,128)} fusion(f32[2048,2816]{1,0:T(8,128)} %fusion.59, f32[2048,2816]{1,0:T(8,128)} %fusion.64, bf16[1,2048,1024]{2,1,0:T(8,128)(2,1)S(1)} %copy-done.3), kind=kOutput, calls=%fused_computation.67 | convolution fusion | flops 11845763072 | bytes 61865984 | tf_op jit(solution)/vmap(transpose(jvp()))/dot_general | solution.py:9
  763.4 447.7 %fusion.107 = (f32[48,1024]{1,0:T(8,128)S(1)}, f32[48,1024]{1,0:T(8,128)S(1)}) fusion(f32[1,2816,1024]{2,1,0:T(8,128)} %convolution_bitcast_fusion, f32[1,2816,1024]{2,1,0:T(8,128)} %fusion.51), kind=kCustom, calls=%all-reduce-scatter.2 | all-reduce-scatter fusion | flops 6291457 | bytes 23462400
  1213.8 1.3 collective-permute-start.1
  1216.4 3.0 collective-permute-start.3
  1219.4 3.4 collective-permute-start.4
  1222.8 1.8 collective-permute-start
  1225.9 5.3 collective-permute-start.7
  1231.2 7.5 collective-permute-start.8
  1238.7 1.9 collective-permute-start.9
  1240.6 1.3 collective-permute-start.10
  1241.9 2.5 collective-permute-start.6
  1244.4 7.6 fusion.76
  1252.1 6.4 copy.12
  1262.8 11.8 reduce-scatter.27.cloned.1.call-done
  1276.2 373.3 %reduce-scatter.23.cloned.1.call-done = f32[1,16,2816]{2,1,0:T(8,128)} async-done(((f32[1,1024,2816]{2,1,0:T(8,128)}), f32[1,16,2816]{2,1,0:T(8,128)}) %reduce-scatter.23.cloned.1.call-update) | async-done | bytes 180240
  1650.5 374.1 %reduce-scatter.21.cloned.1.call-done = f32[1,16,2816]{2,1,0:T(8,128)} async-done(((f32[1,1024,2816]{2,1,0:T(8,128)}), f32[1,16,2816]{2,1,0:T(8,128)}) %reduce-scatter.21.cloned.1.call-update) | async-done | bytes 180240
  (80 shorter events, 17.6 us)
Async XLA Ops:
  7.2 77.1 %all-gather.29.cloned.1.call-start = ((), (), s32[]{:S(2)}) async-start(), calls=%async_computation.4 | async-start | bytes 5857280 | tf_op jit(solution)/vmap(jvp())/squeeze | solution.py:27
  8.9 148.0 %all-gather.31.cloned.1.call-start = ((), (), s32[]{:S(2)}) async-start(), calls=%async_computation.5 | async-start | bytes 5857280 | tf_op jit(solution)/vmap(jvp())/squeeze | solution.py:27
  10.5 236.2 %all-gather.33.cloned.1.call-start = ((), (), s32[]{:S(2)}) async-start(), calls=%async_computation.6 | async-start | bytes 11714560 | tf_op jit(solution)/vmap(jvp())/squeeze | solution.py:27
  12.7 324.7 %all-gather.37.cloned.1.call-start = ((), (), s32[]{:S(2)}) async-start(), calls=%async_computation.8 | async-start | bytes 11714560 | tf_op jit(solution)/vmap(jvp())/squeeze | solution.py:27
  13.2 397.3 %all-gather.35.cloned.1.call-start = ((), (), s32[]{:S(2)}) async-start(), calls=%async_computation.7 | async-start | bytes 5857280 | tf_op jit(solution)/vmap(jvp())/squeeze | solution.py:27
  13.8 469.7 %all-gather.39.cloned.1.call-start = ((), (), s32[]{:S(2)}) async-start(), calls=%async_computation.9 | async-start | bytes 5857280 | tf_op jit(solution)/vmap(jvp())/squeeze | solution.py:27
  14.4 1247.5 %reduce-scatter.25.cloned.1.call-start = ((), (), s32[]{:S(2)}) async-start(), calls=%async_computation.12 | async-start | bytes 11714560
  269.6 0.6 copy-start.4
  270.2 297.4 %copy-start.6 = (f32[1,1,2048]{2,1,0:T(1,128)}, f32[1,1,2048]{2,1,0:T(1,128)S(1)}, u32[]{:S(2)}) copy-start(f32[1,1,2048]{2,1,0:T(1,128)S(1)} %rsqrt.23) | copy-start | bytes 24580
  454.3 820.3 %reduce-scatter.27.cloned.1.call-start = ((), (), s32[]{:S(2)}) async-start(), calls=%async_computation.13 | async-start | bytes 11714560
  548.6 18.9 copy-start.5
  548.6 19.0 copy-start.1
  548.6 19.0 copy-start.2
  570.9 21.6 %copy-start = (bf16[1,1,2048,1024]{2,3,1,0:T(8,128)(2,1)}, bf16[1,1,2048,1024]{2,3,1,0:T(8,128)(2,1)S(1)}, u32[]{:S(2)}) copy-start(bf16[1,1,2048,1024]{2,3,1,0:T(8,128)(2,1)S(1)} %fusion.77) | copy-start | bytes 12582916
  637.2 20.5 %copy-start.9 = (f32[2048]{0:T(1024)S(1)}, f32[2048]{0:T(1024)}, u32[]{:S(2)}) copy-start(f32[2048]{0:T(1024)} %get-tuple-element.34) | copy-start | bytes 24580
  681.7 967.9 %reduce-scatter.23.cloned.1.call-start = ((), (), s32[]{:S(2)}) async-start(), calls=%async_computation.11 | async-start | bytes 11714560
  700.6 0.7 copy-start.7
  700.6 1323.9 %reduce-scatter.21.cloned.1.call-start = ((), (), s32[]{:S(2)}) async-start(), calls=%async_computation.10 | async-start | bytes 11714560
  720.0 19.1 copy-start.3
  763.4 461.3 %copy-start.10 = (u32[128]{0:T(128)S(1)}, u32[128]{0:T(128)}, u32[]{:S(2)}) copy-start(u32[128]{0:T(128)} %constant.180) | copy-start | bytes 1540
  763.4 481.1 %copy-start.8 = (f32[1,1,2048]{2,1,0:T(1,128)S(1)}, f32[1,1,2048]{2,1,0:T(1,128)}, u32[]{:S(2)}) copy-start(f32[1,1,2048]{2,1,0:T(1,128)} %get-tuple-element.33) | copy-start | bytes 24580
  1211.1 8.2 collective-permute-start.5
  1212.4 10.3 collective-permute-start.11
  1213.8 12.1 collective-permute-start.1
  1215.1 16.1 collective-permute-start.2
  1216.4 22.3 %collective-permute-start.3 = (bf16[48,1024]{1,0:T(8,128)(2,1)S(1)}, bf16[48,1024]{1,0:T(8,128)(2,1)S(1)}, u32[]{:S(2)}, u32[]{:S(2)}) collective-permute-start(bf16[48,1024]{1,0:T(8,128)(2,1)S(1)} %convert.69), channel_id=1, source_target_pairs={{0,4},{1,5},{2,6},{3,7},{4,8},{5,9},{6,10},{7,11},{8,12},{9,13},{1... | collective-permute-start | bytes 294920
  1219.4 21.2 %collective-permute-start.4 = (bf16[48,1024]{1,0:T(8,128)(2,1)S(1)}, bf16[48,1024]{1,0:T(8,128)(2,1)S(1)}, u32[]{:S(2)}, u32[]{:S(2)}) collective-permute-start(bf16[48,1024]{1,0:T(8,128)(2,1)S(1)} %convert.69), channel_id=1, source_target_pairs={{0,5},{1,6},{2,7},{3,8},{4,9},{5,10},{6,11},{7,12},{8,13},{9,14},{... | collective-permute-start | bytes 294920
  1222.8 19.2 collective-permute-start
  1225.9 33.7 %collective-permute-start.7 = (bf16[48,1024]{1,0:T(8,128)(2,1)S(1)}, bf16[48,1024]{1,0:T(8,128)(2,1)S(1)}, u32[]{:S(2)}, u32[]{:S(2)}) collective-permute-start(bf16[48,1024]{1,0:T(8,128)(2,1)S(1)} %convert.70), channel_id=1, source_target_pairs={{0,2},{1,3},{2,4},{3,5},{4,6},{5,7},{6,8},{7,9},{8,10},{9,11},{10,... | collective-permute-start | bytes 294920
  1231.2 28.5 %collective-permute-start.8 = (bf16[48,1024]{1,0:T(8,128)(2,1)S(1)}, bf16[48,1024]{1,0:T(8,128)(2,1)S(1)}, u32[]{:S(2)}, u32[]{:S(2)}) collective-permute-start(bf16[48,1024]{1,0:T(8,128)(2,1)S(1)} %convert.70), channel_id=1, source_target_pairs={{0,3},{1,4},{2,5},{3,6},{4,7},{5,8},{6,9},{7,10},{8,11},{9,12},{10... | collective-permute-start | bytes 294920
  1238.7 21.0 %collective-permute-start.9 = (bf16[48,1024]{1,0:T(8,128)(2,1)S(1)}, bf16[48,1024]{1,0:T(8,128)(2,1)S(1)}, u32[]{:S(2)}, u32[]{:S(2)}) collective-permute-start(bf16[48,1024]{1,0:T(8,128)(2,1)S(1)} %convert.70), channel_id=1, source_target_pairs={{0,4},{1,5},{2,6},{3,7},{4,8},{5,9},{6,10},{7,11},{8,12},{9,13},{1... | collective-permute-start | bytes 294920
  1240.6 19.1 collective-permute-start.10
  1241.9 17.7 collective-permute-start.6
Sparse Core Ops, SparseCore 0:
  10.8 73.3 all-gather.28
  87.1 69.6 all-gather.30
  160.3 86.4 all-gather.32
  250.1 87.2 all-gather.36
  340.1 70.4 all-gather.34
  413.9 69.6 all-gather.38
  486.0 384.8 reduce-scatter.24
  873.3 401.2 reduce-scatter.26
  1277.0 372.4 reduce-scatter.22
  1651.8 372.7 reduce-scatter.20
where the time goes:
time: 2040 us; the launch traced here: 2030 us
  waiting for transfers between devices  1070 us (52%)
  blocking collectives  448 us (22%)
  matrix products  355 us (17%)
  other arithmetic  86.6 us (4%)
  starting transfers between devices  32.2 us (2%)
  local copies, waits for them, and re-layouts  29.8 us (1%)
    unnamed x26, waiting for transfers between devices  761 us
    unnamed x1, blocking collectives  448 us
    squeeze x6, waiting for transfers between devices, stack(): h = layer(h, {name: w[number] for name, w in weights.items()})  306 us
    dot_general x6, matrix products, layer(): up = jnp.dot(a, w['w_up'], preferred_element_type=jnp.float32)  130 us
    dot_general x6, matrix products, layer(): gate = jnp.dot(a, w['w_gate'], preferred_element_type=jnp.float32)  117 us
    dot_general x5, matrix products, matmul(): jnp.dot(a, w, preferred_element_type=jnp.float32).astype(jnp.bfloat16)  108 us
    unnamed x5, other arithmetic  66.3 us
  transfers between devices with their start and end apart: 22, of which 9 were waited for; matrix products, arithmetic and copies ran while one was open for 45% of the time, Pallas kernels for 0%

commit v1 on v0

v1 whole, which is shorter than its diff:
```python
import functools
import jax, jax.numpy as jnp
from jax import lax
from jax.experimental import pallas as pl
from jax.experimental.pallas import tpu as pltpu
from jax.sharding import PartitionSpec as P
bf=jnp.bfloat16
MESH=pl.DeviceIdType.MESH
PERM=((0,1,2),(1,2,0),(2,0,1))

def coords():
    i=lax.axis_index("dp")
    return [i//16,(i//4)%4,i%4]

def shifted(me,axis,d):
    c=list(me); c[axis]=(c[axis]+d)%4
    return {"dp":c[0]*16+c[1]*4+c[2]}

def peers(me,far=True):
    return [shifted(me,a,d) for a in range(3) for d in ((1,3,2) if far else (1,3))]

def barrier(me,far=True,sib=True):
    b=pltpu.get_barrier_semaphore()
    n=0
    for t in peers(me,far):
        pl.semaphore_signal(b,inc=1,device_id=t,device_id_type=MESH); n+=1
    if sib:
        pl.semaphore_signal(b,inc=1,device_id={"rep":1-lax.axis_index("rep")},device_id_type=MESH); n+=1
    pl.semaphore_wait(b,n)

class Gather:
    NSEM=15
    def __init__(self,me,own,out,ssem,rsem,lsem,cols):
        self.me,self.own,self.out,self.ssem,self.rsem,self.lsem,self.cols=me,own,out,ssem,rsem,lsem,cols
        self.r=lax.axis_index("rep"); self.sib={"rep":1-self.r}
    def at(self,p,r,u,v,w):
        i=[None]*3
        for a,k in zip(PERM[p],(u,v,w)): i[a]=k
        return self.out.at[(r,*i,slice(None),pl.ds(*self.cols[p]))]
    def copy(self,p,k,src,dst,dev):
        return pltpu.make_async_remote_copy(src_ref=src,dst_ref=dst,send_sem=self.ssem.at[p,k],recv_sem=self.rsem.at[p,k],device_id=dev,device_id_type=MESH)
    def m(self,p,k): return self.me[PERM[p][k]]
    def sent(self,p,k):
        r=self.r; u,v,w=(self.m(p,j) for j in range(3)); A=slice(None); lo,hi=pl.ds(0,2),pl.ds(2,2)
        ax=PERM[p]
        me=self.me
        if k<3:
            src=self.own.at[r,:,pl.ds(*self.cols[p])]; dst=self.at(p,r,u,v,w)
            return src,dst,shifted(me,ax[0],(1,3,2)[k])
        if k<5:
            ref=self.at(p,r,A,v,w); return ref,ref,shifted(me,ax[1],(1,3)[k-3])
        if k==5: ref=self.at(p,r,lo,(v+3)%4,w); return ref,ref,shifted(me,ax[1],1)
        if k==6: ref=self.at(p,r,hi,(v+1)%4,w); return ref,ref,shifted(me,ax[1],3)
        if k<9:
            ref=self.at(p,r,A,A,w); return ref,ref,shifted(me,ax[2],(1,3)[k-7])
        if k==9: ref=self.at(p,r,lo,A,(w+3)%4); return ref,ref,shifted(me,ax[2],1)
        if k==10: ref=self.at(p,r,hi,A,(w+1)%4); return ref,ref,shifted(me,ax[2],3)
        ref=self.at(p,r,A,A,(w+(0,3,1,2)[k-11])%4); return ref,ref,self.sib
    def received(self,p,k):
        r=self.r; u,v,w=(self.m(p,j) for j in range(3)); A=slice(None); lo,hi=pl.ds(0,2),pl.ds(2,2)
        if k<3: return self.at(p,r,(u+(3,1,2)[k])%4,v,w)
        if k<5: return self.at(p,r,A,(v+(3,1)[k-3])%4,w)
        if k==5: return self.at(p,r,lo,(v+2)%4,w)
        if k==6: return self.at(p,r,hi,(v+2)%4,w)
        if k<9: return self.at(p,r,A,A,(w+(3,1)[k-7])%4)
        if k==9: return self.at(p,r,lo,A,(w+2)%4)
        if k==10: return self.at(p,r,hi,A,(w+2)%4)
        return self.at(p,1-r,A,A,(w+(0,3,1,2)[k-11])%4)
    def start(self,p,k):
        s,d,dev=self.sent(p,k); self.copy(p,k,s,d,dev).start()
    def wait_send(self,p,k):
        s,d,dev=self.sent(p,k); self.copy(p,k,s,d,dev).wait_send()
    def wait_recv(self,p,k):
        ref=self.received(p,k); self.copy(p,k,ref,ref,self.sib).wait_recv()
    def local(self,p):
        return pltpu.make_async_copy(self.own.at[self.r,:,pl.ds(*self.cols[p])],self.at(p,self.r,*(self.m(p,j) for j in range(3))),self.lsem.at[p])
    def events(self):
        P3=range(3)
        def e0():
            for p in P3:
                self.local(p).start()
                for k in (0,1,2): self.start(p,k)
        def e1():
            for p in P3:
                self.local(p).wait()
                for k in (0,1,2): self.wait_recv(p,k)
                for k in (3,4): self.start(p,k)
        def e2():
            for p in P3:
                for k in (3,4): self.wait_recv(p,k); self.start(p,k+2)
        def e3():
            for p in P3:
                for k in (5,6): self.wait_recv(p,k)
                for k in (7,8,11): self.start(p,k)
        def e4():
            for p in P3:
                for k in (7,8): self.wait_recv(p,k); self.start(p,k+2); self.start(p,k+5)
        def e5():
            for p in P3:
                for k in (9,10): self.wait_recv(p,k)
                self.start(p,14)
        def e6():
            for p in P3:
                for k in range(15): self.wait_send(p,k)
                for k in range(11,15): self.wait_recv(p,k)
        return [e0,e1,e2,e3,e4,e5,e6]

f32=jnp.float32

class Scatter:
    N1,N2,N3=6,6,3
    NSEM=15
    @staticmethod
    def scratch(R,cols):
        s=[]
        for p in range(3):
            n=cols[p][1]
            h=Scatter.half_shape(p)
            s+=[pltpu.VMEM((6,*h,R,n),bf),
                pltpu.VMEM((4,*h,R,n),bf),
                pltpu.VMEM((4,4,R,n),f32),pltpu.VMEM((4,4,R,n),bf),
                pltpu.VMEM((6,2,R,n),bf),pltpu.VMEM((2,2,R,n),bf),
                pltpu.VMEM((4,R,n),f32),pltpu.VMEM((4,R,n),bf),
                pltpu.VMEM((3,R,n),bf)]
        return s+[pltpu.VMEM((R,sum(c[1] for c in cols)),bf),pltpu.SemaphoreType.DMA((3,15)),pltpu.SemaphoreType.DMA((3,15)),pltpu.SemaphoreType.DMA((3,4)),pltpu.SemaphoreType.DMA(())]
    @staticmethod
    def half_shape(p):
        _,v,w=PERM[p]
        return (2,4) if v<w else (4,2)
    def __init__(self,me,g,out,bufs,cols):
        self.me,self.g,self.out,self.cols=me,g,out,cols
        self.b=[bufs[9*p:9*p+9] for p in range(3)]
        self.res,self.ssem,self.rsem,self.lsem,self.osem=bufs[27:]
    def m(self,p,k,d=0): return (self.me[PERM[p][k]]+d)%4
    def gat(self,p,u,half):
        i=[None]*3
        _,v,w=PERM[p]
        i[PERM[p][0]]=u; i[v]=pl.ds(2*half,2); i[w]=slice(None)
        return self.g.at[(*i,slice(None),pl.ds(*self.cols[p]))]
    def hidx(self,p,v,w):
        _,a,b=PERM[p]
        return (v,w) if a<b else (w,v)
    def own(self,p,j):
        u,h=((1,0),(3,1),(0,0),(0,1))[j]
        return pltpu.make_async_copy(self.gat(p,self.m(p,0,u),h),self.b[p][1].at[j],self.lsem.at[p,j])
    def rc(self,p,k,src,dst,ax,d):
        return pltpu.make_async_remote_copy(src_ref=src,dst_ref=dst,send_sem=self.ssem.at[p,k],recv_sem=self.rsem.at[p,k],device_id=shifted(self.me,PERM[p][ax],d),device_id_type=MESH)
    def cp(self,p,k):
        b=self.b[p]
        if k<6:
            d=(1,3,1,3,1,3)[k]
            if k<4:
                u,h=((2,0),(2,1),(1,1),(3,0))[k]
                src=self.gat(p,self.m(p,0,u),h)
            else: src=b[1].at[k-4]
            return self.rc(p,k,src,b[0].at[k],0,d)
        if k<12:
            j=k-6; d=(1,3,1,3,1,3)[j]
            if j<4:
                v,h=((2,0),(2,1),(1,1),(3,0))[j]
                src=b[3].at[self.m(p,1,v),pl.ds(2*h,2)]
            else: src=b[5].at[j-4]
            return self.rc(p,k,src,b[4].at[j],1,d)
        j=k-12; d=(1,3,2)[j]
        return self.rc(p,k,b[7].at[self.m(p,2,d)],b[8].at[j],2,d)
    def events(self):
        P3=range(3)
        def e0():
            for k in (0,1,2,3):
                for p in P3: self.cp(p,k).start()
            for p in P3:
                for j in range(4): self.own(p,j).start()
        def e1():
            for p in P3:
                b=self.b[p]; h=self.half_shape(p)
                for k in (0,1):
                    self.own(p,k).wait(); self.cp(p,k).wait_recv()
                    def add(i,_,b=b,h=h,k=k):
                        ix=(k,i//h[1],i%h[1])
                        b[1][ix]=(b[0][ix].astype(f32)+b[1][ix].astype(f32)).astype(bf)
                        return 0
                    lax.fori_loop(0,8,add,0)
            for p in P3:
                for k in (4,5): self.cp(p,k).start()
        def e2():
            for p in P3:
                b=self.b[p]
                for k in (2,3,4,5): self.cp(p,k).wait_recv()
                for j in (2,3): self.own(p,j).wait()
                for hf in (0,1):
                    own,sm,raw=((2,4,3),(3,5,2))[hf]
                    def add(i,_,b=b,hf=hf,own=own,sm=sm,raw=raw,p=p):
                        v,w=i//4,i%4
                        ix=self.hidx(p,v,w)
                        t=b[1][(own,*ix)].astype(f32)+b[0][(sm,*ix)].astype(f32)+b[0][(raw,*ix)].astype(f32)
                        b[2][2*hf+v,w]=t; b[3][2*hf+v,w]=t.astype(bf)
                        return 0
                    lax.fori_loop(0,8,add,0)
        def e3():
            for k in (6,7,8,9):
                for p in P3: self.cp(p,k).start()
        def e4():
            for p in P3:
                b=self.b[p]
                for hf in (0,1):
                    self.cp(p,6+hf).wait_recv()
                    v=self.m(p,1,(1,3)[hf])
                    for w in (0,1):
                        b[5][hf,w]=(b[4][hf,w].astype(f32)+b[2][v,2*hf+w]).astype(bf)
            for p in P3:
                for k in (10,11): self.cp(p,k).start()
        def e5():
            for p in P3:
                b=self.b[p]; v=self.m(p,1)
                for k in (8,9,10,11): self.cp(p,k).wait_recv()
                for hf in (0,1):
                    sm,raw=((4,3),(5,2))[hf]
                    for w in (0,1):
                        t=b[2][v,2*hf+w]+b[4][sm,w].astype(f32)+b[4][raw,w].astype(f32)
                        b[6][2*hf+w]=t; b[7][2*hf+w]=t.astype(bf)
        def e6():
            for k in (12,13,14):
                for p in P3: self.cp(p,k).start()
        def e7():
            for p in P3:
                b=self.b[p]; w=self.m(p,2)
                for k in (12,13,14): self.cp(p,k).wait_recv()
                t=b[6][w]
                for j in range(3): t=t+b[8][j].astype(f32)
                self.res[:,pl.ds(*self.cols[p])]=t.astype(bf)
            pltpu.make_async_copy(self.res,self.out,self.osem).start()
            for p in P3:
                for k in range(15): self.cp(p,k).wait_send()
            pltpu.make_async_copy(self.res,self.out,self.osem).wait()
        return [e0,e1,e2,e3,e4,e5,e6,e7]

NAMES = ("w_gate", "w_up", "w_down")
GU_COLS = ((0, 1024), (1024, 896), (1920, 896))
D_COLS = ((0, 384), (384, 384), (768, 256))


def gather_call(pair, cols, number):
    rows, width = pair.shape[1:]

    def kernel(own, out, *sems):
        me = coords()
        barrier(me)
        for event in Gather(me, own, out, *sems, cols).events():
            event()

    return pl.pallas_call(
        kernel,
        in_specs=[pl.BlockSpec(memory_space=pltpu.VMEM)],
        out_specs=pl.BlockSpec(memory_space=pltpu.HBM),
        out_shape=jax.ShapeDtypeStruct((2, 4, 4, 4, rows, width), bf),
        scratch_shapes=[pltpu.SemaphoreType.DMA((3, 15)), pltpu.SemaphoreType.DMA((3, 15)), pltpu.SemaphoreType.DMA((3,))],
        compiler_params=pltpu.CompilerParams(collective_id=number, has_side_effects=True),
        name=f"gather_{number}",
    )(pair)


def scatter_call(g, cols, number):
    rows, width = g.shape[3:]

    def kernel(g, out, *bufs):
        me = coords()
        barrier(me, sib=False)
        for event in Scatter(me, g, out, bufs, cols).events():
            event()

    return pl.pallas_call(
        kernel,
        in_specs=[pl.BlockSpec(memory_space=pltpu.HBM)],
        out_specs=pl.BlockSpec(memory_space=pltpu.HBM),
        out_shape=jax.ShapeDtypeStruct((rows, width), bf),
        scratch_shapes=Scatter.scratch(rows, cols),
        compiler_params=pltpu.CompilerParams(collective_id=number, has_side_effects=True, vmem_limit_bytes=60 * 2**20),
        name=f"scatter_{number}",
    )(g)


def matmul(a, w):
    return jnp.dot(a, w, preferred_element_type=f32).astype(bf)


def normed(h):
    wide = h.astype(f32)
    scale = lax.rsqrt(jnp.mean(wide**2, -1, keepdims=True) + 1e-6)
    return (wide * scale).astype(bf)


def layer(h, w):
    a = normed(h)
    gate = jnp.dot(a, w["w_gate"], preferred_element_type=f32)
    up = jnp.dot(a, w["w_up"], preferred_element_type=f32)
    return h + matmul((jax.nn.silu(gate) * up).astype(bf), w["w_down"])


def stack(weights, h):
    for w in weights:
        h = layer(h, w)
    return h


def solution(mesh):
    def device(x, dy, w_gate, w_up, w_down):
        gu = [gather_call(jnp.stack([w_gate[n], w_up[n]]), GU_COLS, n).reshape(2, 1024, 2816) for n in (0, 1)]
        dd = gather_call(w_down, D_COLS, 2).reshape(2, 2816, 1024)
        weights = [dict(zip(NAMES, (*gu[n], dd[n]), strict=True)) for n in (0, 1)]
        _, back = jax.vjp(stack, weights, x[0])
        by_weights, by_x = back(dy[0])
        outs = []
        for j, name in enumerate(NAMES):
            rows, cols = (44, D_COLS) if name == "w_down" else (16, GU_COLS)
            both = [scatter_call(by_weights[n][name].reshape(4, 4, 4, rows, -1), cols, 3 + 2 * j + n) for n in (0, 1)]
            outs.append(jnp.stack(both))
        return (by_x[None], *outs)

    return jax.shard_map(
        device,
        mesh=mesh,
        in_specs=(P(("rep", "dp")), P(("rep", "dp")), *(P(None, "dp"),) * 3),
        out_specs=(P(("rep", "dp")), *(P("rep", "dp"),) * 3),
        check_vma=False,
    )
```

time: 2040 us -> 819 us (0.40)
  waiting for transfers between devices: 1070 us -> 0 us
  blocking collectives: 448 us -> 0 us
  Pallas kernels: 0 us -> 322 us
  other arithmetic: 86.6 us -> 18.8 us
  local copies, waits for them, and re-layouts: 29.8 us -> 90.5 us
  starting transfers between devices: 32.2 us -> 0 us
  matrix products: 355 us -> 377 us
    unnamed x26 -> x0, waiting for transfers between devices: 761 us -> none
    unnamed x1 -> x0, blocking collectives: 448 us -> none
    pallas_call x0 -> x9, Pallas kernels: none -> 322 us  [the longest x6 198 us: scatter_call(): pl.pallas_call(kernel, in_specs=[pl.BlockSpec(memory_space=pltpu.HBM)], o...]
    squeeze x6 -> x0, waiting for transfers between devices: 306 us -> none  [stack(): h = layer(h, {name: w[number] for name, w in weights.items()})]
    unnamed x5 -> x1, other arithmetic: 66.3 us -> 0.01 us
    unnamed x16 -> x0, starting transfers between devices: 32 us -> none
    dot_general x17, matrix products: 355 us -> 377 us  [the longest x6 135 us: layer(): up = jnp.dot(a, w['w_up'], preferred_element_type=f32)]
  transfers between devices with their start and end apart: 22 -> 0, of which waited for: 9 -> 0; matrix products, arithmetic and copies ran while one was open for 45% -> 0% of each run, Pallas kernels for 0% -> 0%
where the time goes in v1:
time: 819 us; the launch traced here: 809 us
  matrix products  377 us (46%)
  Pallas kernels  322 us (39%)
  local copies, waits for them, and re-layouts  90.5 us (11%)
  other arithmetic  18.8 us (2%)
    pallas_call x6, Pallas kernels, scatter_call(): pl.pallas_call(kernel, in_specs=[pl.BlockSpec(memory_space=pltpu.HBM)], o...  198 us
    dot_general x6, matrix products, layer(): up = jnp.dot(a, w['w_up'], preferred_element_type=f32)  135 us
    dot_general x6, matrix products, layer(): gate = jnp.dot(a, w['w_gate'], preferred_element_type=f32)  130 us
    pallas_call x3, Pallas kernels, gather_call(): pl.pallas_call(kernel, in_specs=[pl.BlockSpec(memory_space=pltpu.VMEM)],...  124 us
    dot_general x5, matrix products, matmul(): return jnp.dot(a, w, preferred_element_type=f32).astype(bf)  112 us
    unnamed x45, local copies, waits for them, and re-layouts  23 us
    another operation x2, local copies, waits for them, and re-layouts, device(): weights = [dict(zip(NAMES, (*gu[n], dd[n]), strict=True)) for n in (0, 1)]  19.5 us
    reshape x2, local copies, waits for them, and re-layouts, device(): by_weights[n][name].reshape(4, 4, 4, rows, -1)  18.4 us

profile of v1, /device:TPU:0, one launch (start us, length us, event | category | flops | bytes accessed | tf_op | source)
XLA Modules:
  0.0 808.9 jit_solution(13741744019315842848)
XLA Ops:
  0.7 6.5 copy.15
  7.1 3.1 fusion.15
  10.2 0.0 copy-start.12
  10.3 0.0 copy-done.8
  10.3 0.8 pad_maximum_fusion.1
  11.1 42.2 %gather_0.1 = bf16[2,4,4,4,16,2816]{5,4,3,2,1,0:T(8,128)(2,1)} custom-call(bf16[2,16,2816]{2,1,0:T(8,128)(2,1)} %get-tuple-element.34.own), custom_call_target="tpu_custom_call" | custom-call | tf_op jit(solution)/shard_map/gather_0/pallas_call | solution.py:251
  53.3 9.8 %fusion.51 = (bf16[1,4,4,4,16,2816]{5,4,3,2,1,0:T(8,128)(2,1)}, bf16[1,4,4,4,16,2816]{5,4,3,2,1,0:T(8,128)(2,1)}) fusion(bf16[2,4,4,4,16,2816]{5,4,3,2,1,0:T(8,128)(2,1)} %gather_0.1), kind=kLoop, calls=%fused_computation.76 | loop fusion | bytes 23068672 | tf_op jit(solution)/shard_map/unstack | solution.py:309
  63.0 20.0 %fusion.40 = f32[2048,2816]{1,0:T(8,128)} fusion(bf16[1024,2816]{1,0:T(8,128)(2,1)} %bitcast.61, bf16[1,2048,1024]{2,1,0:T(8,128)(2,1)} %param.5, f32[2048]{0:T(1024)S(1)} %fusion.42), kind=kOutput, calls=%fused_computation.62 | convolution fusion | flops 11817451520 | bytes 33038336 | tf_op jit(solution)/shard_map/jvp()/dot_general | solution.py:294
  83.1 26.9 %multiply_convert_fusion.1 = (bf16[2048,2816]{1,0:T(8,128)(2,1)}, f32[2048,2816]{1,0:T(8,128)}) fusion(f32[2048,2816]{1,0:T(8,128)} %fusion.40, bf16[1024,2816]{1,0:T(8,128)(2,1)S(1)} %bitcast.64, bf16[1,2048,1024]{2,1,0:T(8,128)(2,1)} %param.5, f32[2048]{0:T(1024)S(1)} %fusion.42), kind=kOutput, calls=%fused_computation.13 | convolution fusion | flops 11852054528 | bytes 67641344 | tf_op jit(solution)/shard_map/jvp()/dot_general | solution.py:295
  109.9 0.7 copy.16.own
  110.7 40.4 %gather_2.1 = bf16[2,4,4,4,44,1024]{5,4,3,2,1,0:T(8,128)(2,1)} custom-call(bf16[2,44,1024]{2,1,0:T(8,128)(2,1)} %copy.16.own), custom_call_target="tpu_custom_call" | custom-call | tf_op jit(solution)/shard_map/gather_2/pallas_call | solution.py:251
  151.0 11.2 %fusion.49 = (bf16[1,4,4,4,44,1024]{5,4,3,2,1,0:T(8,128)(2,1)}, bf16[1,4,4,4,44,1024]{5,4,3,2,1,0:T(8,128)(2,1)}) fusion(bf16[2,4,4,4,44,1024]{5,4,3,2,1,0:T(8,128)(2,1)} %gather_2.1), kind=kLoop, calls=%fused_computation.74 | loop fusion | bytes 23068672 | tf_op jit(solution)/shard_map/slice | solution.py:309
  162.2 9.1 %squeeze.14 = bf16[2816,1024]{1,0:T(8,128)(2,1)} reshape(bf16[1,4,4,4,44,1024]{5,4,3,2,1,0:T(8,128)(2,1)} %get-tuple-element.13) | data formatting | bytes 11534336 | tf_op jit(solution)/shard_map/squeeze | solution.py:309
  171.4 19.4 %fusion.18 = (f32[2048]{0:T(1024)S(1)}, bf16[2048,1024]{0,1:T(8,128)(2,1)}) fusion(bf16[2048,2816]{1,0:T(8,128)(2,1)} %get-tuple-element.22, bf16[2816,1024]{1,0:T(8,128)(2,1)} %squeeze.14, bf16[1,2048,1024]{1,2,0:T(8,128)(2,1)} %copy.15), kind=kOutput, calls=%fused_computation.40 | convolution fusion | flops 11821643776 | bytes 25698304 | tf_op jit(solution)/shard_map/jvp()/dot_general | solution.py:283
  190.8 41.0 %gather_1.1 = bf16[2,4,4,4,16,2816]{5,4,3,2,1,0:T(8,128)(2,1)} custom-call(bf16[2,16,2816]{2,1,0:T(8,128)(2,1)} %get-tuple-element.35.own), custom_call_target="tpu_custom_call" | custom-call | tf_op jit(solution)/shard_map/gather_1/pallas_call | solution.py:251
  231.8 9.8 %fusion.50 = (bf16[1,4,4,4,16,2816]{5,4,3,2,1,0:T(8,128)(2,1)}, bf16[1,4,4,4,16,2816]{5,4,3,2,1,0:T(8,128)(2,1)}) fusion(bf16[2,4,4,4,16,2816]{5,4,3,2,1,0:T(8,128)(2,1)} %gather_1.1), kind=kLoop, calls=%fused_computation.75 | loop fusion | bytes 23068672 | tf_op jit(solution)/shard_map/unstack | solution.py:309
  241.6 20.1 %fusion.34 = f32[2048,2816]{1,0:T(8,128)} fusion(bf16[1024,2816]{1,0:T(8,128)(2,1)} %bitcast.69, bf16[2048,1024]{0,1:T(8,128)(2,1)} %get-tuple-element.25, f32[2048]{0:T(1024)S(1)} %fusion.43), kind=kOutput, calls=%fused_computation.59 | convolution fusion | flops 11817451520 | bytes 33038336 | tf_op jit(solution)/shard_map/jvp()/dot_general | solution.py:295
  261.7 9.2 %squeeze.15 = bf16[2816,1024]{1,0:T(8,128)(2,1)} reshape(bf16[1,4,4,4,44,1024]{5,4,3,2,1,0:T(8,128)(2,1)} %get-tuple-element.12) | data formatting | bytes 11534336 | tf_op jit(solution)/shard_map/squeeze | solution.py:309
  270.9 18.3 %convolution_convert_fusion.1 = bf16[2048,2816]{1,0:T(8,128)(2,1)} fusion(bf16[2816,1024]{1,0:T(8,128)(2,1)} %squeeze.15, bf16[1,2048,1024]{2,1,0:T(8,128)(2,1)} %param.6), kind=kOutput, calls=%fused_computation.30 | convolution fusion | flops 11816927232 | bytes 21495808 | tf_op jit(solution)/shard_map/transpose(jvp())/dot_general | solution.py:283
  289.2 33.0 %fusion.1 = (bf16[2048,2816]{1,0:T(8,128)(2,1)}, f32[2048,2816]{1,0:T(8,128)}) fusion(f32[2048,2816]{1,0:T(8,128)} %fusion.34, bf16[2048,2816]{1,0:T(8,128)(2,1)} %convolution_convert_fusion.1, bf16[1024,2816]{1,0:T(8,128)(2,1)S(1)} %bitcast.68, bf16[2048,1024]{0,1:T(8,128)(2,1)} %get-tuple-element.25, f32[2048]{0:T(1024)S(1)} %fusion.43), kind=kOutput, calls=%fused_computation.7 | convolution fusion | flops 11886657536 | bytes 79175680 | tf_op jit(solution)/shard_map/jvp()/dot_general | solution.py:294
  322.2 21.5 %fusion.7 = bf16[2048,1024]{0,1:T(8,128)(2,1)} fusion(bf16[1024,2816]{1,0:T(8,128)(2,1)} %bitcast.70, bf16[2048,2816]{1,0:T(8,128)(2,1)} %convolution_convert_fusion.1, f32[2048,2816]{1,0:T(8,128)} %get-tuple-element.27), kind=kOutput, calls=%fused_computation.17 | convolution fusion | flops 11845763072 | bytes 44564480 | tf_op jit(solution)/shard_map/transpose(jvp())/dot_general | solution.py:295
  343.7 20.3 %fusion.20 = (f32[2048]{0:T(1024)S(1)}, bf16[2048,1024]{0,1:T(8,128)(2,1)}) fusion(bf16[2048,1024]{0,1:T(8,128)(2,1)} %get-tuple-element.25, bf16[2048,1024]{0,1:T(8,128)(2,1)} %fusion.7, bf16[2048,2816]{1,0:T(8,128)(2,1)} %get-tuple-element.26, bf16[1024,2816]{1,0:T(8,128)(2,1)} %bitcast.65), kind=kOutput, calls=%fused_computation.42 | convolution fusion | flops 11821643776 | bytes 29892608 | tf_op jit(solution)/shard_map/transpose(jvp())/dot_general | solution.py:294
  364.0 6.5 copy.14
  370.5 6.2 fusion.27
  376.7 1.9 copy-done.1
  378.7 16.8 %convolution_convert_fusion.2 = bf16[2816,1024]{1,0:T(8,128)(2,1)} fusion(bf16[2048,2816]{1,0:T(8,128)(2,1)} %get-tuple-element.22, bf16[2048,1024]{0,1:T(8,128)(2,1)S(1)} %fusion.27), kind=kOutput, calls=%fused_computation.47 | convolution fusion | flops 11814043648 | bytes 21495808 | tf_op jit(solution)/shard_map/transpose(jvp())/dot_general | solution.py:283
  395.5 9.3 %reshape.93.g = bf16[4,4,4,44,1024]{4,3,2,1,0:T(8,128)(2,1)} reshape(bf16[2816,1024]{1,0:T(8,128)(2,1)} %convolution_convert_fusion.2) | data formatting | bytes 11534336 | tf_op jit(solution)/shard_map/reshape | solution.py:315
  404.7 40.4 %scatter_7.1 = bf16[44,1024]{1,0:T(8,128)(2,1)} custom-call(bf16[4,4,4,44,1024]{4,3,2,1,0:T(8,128)(2,1)} %reshape.93.g), custom_call_target="tpu_custom_call" | custom-call | tf_op jit(solution)/shard_map/scatter_7/pallas_call | solution.py:271
  445.1 23.7 %fusion.21 = bf16[2816,1024]{1,0:T(8,128)(2,1)} fusion(f32[2048,2816]{1,0:T(8,128)} %fusion.34, bf16[1,2048,1024]{2,1,0:T(8,128)(2,1)} %param.6, f32[2048,2816]{1,0:T(8,128)} %get-tuple-element.27), kind=kOutput, calls=%fused_computation.44 | convolution fusion | flops 11848646656 | bytes 56098816 | tf_op jit(solution)/shard_map/transpose(jvp())/dot_general | solution.py:283
  468.8 9.1 %reshape.94.g = bf16[4,4,4,44,1024]{4,3,2,1,0:T(8,128)(2,1)} reshape(bf16[2816,1024]{1,0:T(8,128)(2,1)} %fusion.21) | data formatting | bytes 11534336 | tf_op jit(solution)/shard_map/reshape | solution.py:315
  477.9 35.6 %scatter_8.1 = bf16[44,1024]{1,0:T(8,128)(2,1)} custom-call(bf16[4,4,4,44,1024]{4,3,2,1,0:T(8,128)(2,1)} %reshape.94.g), custom_call_target="tpu_custom_call" | custom-call | tf_op jit(solution)/shard_map/scatter_8/pallas_call | solution.py:271
  513.6 0.9 pad_maximum_fusion
  514.5 0.9 copy.18
  515.4 33.9 %fusion.3 = (bf16[2048,2816]{1,0:T(8,128)(2,1)}, bf16[2048,2816]{1,0:T(8,128)(2,1)}) fusion(f32[2048,2816]{1,0:T(8,128)} %fusion.40, f32[2048,2816]{1,0:T(8,128)} %get-tuple-element.23, bf16[2048,1024]{0,1:T(8,128)(2,1)} %copy-done.1, bf16[2816,1024]{1,0:T(8,128)(2,1)} %squeeze.14), kind=kOutput, calls=%fused_computation.9 | convolution fusion | flops 11886133248 | bytes 79167488 | tf_op jit(solution)/shard_map/transpose(jvp())/dot_general | solution.py:283
  549.3 22.4 %fusion.22 = bf16[1024,2816]{1,0:T(8,128)(2,1)} fusion(bf16[2048,2816]{1,0:T(8,128)(2,1)} %get-tuple-element.31, bf16[1,2048,1024]{1,2,0:T(8,128)(2,1)} %copy.15, f32[2048]{0:T(1024)S(1)} %copy-done.13, f32[2048,2816]{1,0:T(8,128)} %fusion.40), kind=kOutput, calls=%fused_computation.45 | convolution fusion | flops 11854938112 | bytes 44572672 | tf_op jit(solution)/shard_map/transpose(jvp())/dot_general | solution.py:295
  571.8 31.1 %scatter_5.1 = bf16[16,2816]{1,0:T(8,128)(2,1)} custom-call(bf16[4,4,4,16,2816]{4,3,2,1,0:T(8,128)(2,1)} %bitcast.59), custom_call_target="tpu_custom_call" | custom-call | tf_op jit(solution)/shard_map/scatter_5/pallas_call | solution.py:271
  602.8 22.5 %fusion.23 = bf16[1024,2816]{1,0:T(8,128)(2,1)} fusion(bf16[2048,2816]{1,0:T(8,128)(2,1)} %convolution_convert_fusion.1, bf16[2048,1024]{0,1:T(8,128)(2,1)} %get-tuple-element.25, f32[2048]{0:T(1024)S(1)} %copy-done.15, f32[2048,2816]{1,0:T(8,128)} %get-tuple-element.27), kind=kOutput, calls=%fused_computation.46 | convolution fusion | flops 11854938112 | bytes 44572672 | tf_op jit(solution)/shard_map/transpose(jvp())/dot_general | solution.py:295
  625.3 31.1 %scatter_6.1 = bf16[16,2816]{1,0:T(8,128)(2,1)} custom-call(bf16[4,4,4,16,2816]{4,3,2,1,0:T(8,128)(2,1)} %bitcast.58), custom_call_target="tpu_custom_call" | custom-call | tf_op jit(solution)/shard_map/scatter_6/pallas_call | solution.py:271
  656.4 1.6 pad_maximum_fusion.4
  658.0 18.6 %convolution_convert_fusion.3 = bf16[1024,2816]{1,0:T(8,128)(2,1)} fusion(bf16[2048,2816]{1,0:T(8,128)(2,1)} %get-tuple-element.26, bf16[2048,1024]{0,1:T(8,128)(2,1)} %get-tuple-element.25, f32[2048]{0:T(1024)S(1)} %copy-done.15), kind=kOutput, calls=%fused_computation.48 | convolution fusion | flops 11817451520 | bytes 21504000 | tf_op jit(solution)/shard_map/transpose(jvp())/dot_general | solution.py:294
  676.5 30.1 %scatter_4.1 = bf16[16,2816]{1,0:T(8,128)(2,1)} custom-call(bf16[4,4,4,16,2816]{4,3,2,1,0:T(8,128)(2,1)} %bitcast.57), custom_call_target="tpu_custom_call" | custom-call | tf_op jit(solution)/shard_map/scatter_4/pallas_call | solution.py:271
  706.6 18.7 %convolution_convert_fusion.4 = bf16[1024,2816]{1,0:T(8,128)(2,1)} fusion(bf16[2048,2816]{1,0:T(8,128)(2,1)} %get-tuple-element.30, bf16[1,2048,1024]{1,2,0:T(8,128)(2,1)} %copy.15, f32[2048]{0:T(1024)S(1)} %copy-done.13), kind=kOutput, calls=%fused_computation.49 | convolution fusion | flops 11817451520 | bytes 21504000 | tf_op jit(solution)/shard_map/transpose(jvp())/dot_general | solution.py:294
  725.3 29.9 %scatter_3.1 = bf16[16,2816]{1,0:T(8,128)(2,1)} custom-call(bf16[4,4,4,16,2816]{4,3,2,1,0:T(8,128)(2,1)} %bitcast.60), custom_call_target="tpu_custom_call" | custom-call | tf_op jit(solution)/shard_map/scatter_3/pallas_call | solution.py:271
  755.1 1.6 pad_maximum_fusion.3
  756.7 21.5 %fusion.9 = bf16[2048,1024]{0,1:T(8,128)(2,1)} fusion(bf16[1024,2816]{1,0:T(8,128)(2,1)} %bitcast.63, bf16[2048,2816]{1,0:T(8,128)(2,1)} %get-tuple-element.31, f32[2048,2816]{1,0:T(8,128)} %fusion.40), kind=kOutput, calls=%fused_computation.19 | convolution fusion | flops 11845763072 | bytes 44564480 | tf_op jit(solution)/shard_map/transpose(jvp())/dot_general | solution.py:295
  778.3 19.1 %fusion.16 = (f32[2048]{0:T(1024)S(1)}, bf16[2048,1024]{0,1:T(8,128)(2,1)S(1)}) fusion(bf16[1,2048,1024]{1,2,0:T(8,128)(2,1)} %copy.15, bf16[2048,1024]{0,1:T(8,128)(2,1)} %fusion.9, bf16[2048,2816]{1,0:T(8,128)(2,1)} %get-tuple-element.30, bf16[1024,2816]{1,0:T(8,128)(2,1)} %bitcast.62), kind=kOutput, calls=%fused_computation.38 | convolution fusion | flops 11821643776 | bytes 29892608 | tf_op jit(solution)/shard_map/transpose(jvp())/dot_general | solution.py:294
  797.4 4.6 fusion.26
  802.1 6.4 copy.17
  (44 shorter events, 0.1 us)
Async XLA Ops:
  0.6 9.6 %copy-start.7 = (bf16[2,16,2816]{2,1,0:T(8,128)(2,1)S(1)}, bf16[2,16,2816]{2,1,0:T(8,128)(2,1)}, u32[]{:S(2)}) copy-start(bf16[2,16,2816]{2,1,0:T(8,128)(2,1)} %param.7) | copy-start | bytes 540676
  0.6 9.6 %copy-start.8 = (bf16[2,16,2816]{2,1,0:T(8,128)(2,1)S(1)}, bf16[2,16,2816]{2,1,0:T(8,128)(2,1)}, u32[]{:S(2)}) copy-start(bf16[2,16,2816]{2,1,0:T(8,128)(2,1)} %param.8) | copy-start | bytes 540676
  10.2 0.9 copy-start.10
  10.2 72.8 %copy-start.12 = (f32[2048]{0:T(1024)}, f32[2048]{0:T(1024)S(1)}, u32[]{:S(2)}) copy-start(f32[2048]{0:T(1024)S(1)} %fusion.42) | copy-start | bytes 24580
  63.0 20.0 %copy-start.3 = (bf16[1,4,4,4,16,2816]{5,4,3,2,1,0:T(8,128)(2,1)S(1)}, bf16[1,4,4,4,16,2816]{5,4,3,2,1,0:T(8,128)(2,1)}, u32[]{:S(2)}) copy-start(bf16[1,4,4,4,16,2816]{5,4,3,2,1,0:T(8,128)(2,1)} %get-tuple-element.17) | copy-start | bytes 17301508
  83.0 26.9 %copy-start.9 = (bf16[2,44,1024]{2,0,1:T(2,128)(2,1)S(1)}, bf16[2,44,1024]{2,0,1:T(2,128)(2,1)}, u32[]{:S(2)}) copy-start(bf16[2,44,1024]{2,0,1:T(2,128)(2,1)} %param.9) | copy-start | bytes 540676
  190.8 50.8 %copy-start.16 = (f32[2048]{0:T(1024)}, f32[2048]{0:T(1024)S(1)}, u32[]{:S(2)}) copy-start(f32[2048]{0:T(1024)S(1)} %get-tuple-element.24) | copy-start | bytes 24580
  190.8 179.7 %copy-start.14 = (f32[2048]{0:T(1024)}, f32[2048]{0:T(1024)S(1)}, u32[]{:S(2)}) copy-start(f32[2048]{0:T(1024)S(1)} %fusion.43) | copy-start | bytes 24580
  261.7 27.5 %slice-start = ((s8[5767168]{0:T(1024)(128)(4,1)}), s8[1572864]{0:T(1024)(128)(4,1)S(1)}, s32[]{:S(2)}) async-start(s8[5767168]{0:T(1024)(128)(4,1)} %bitcast.66), calls=%async_computation | async-start | bytes 3145728
  270.9 18.3 %slice-start.1 = ((s8[5767168]{0:T(1024)(128)(4,1)}), s8[4194304]{0:T(1024)(128)(4,1)S(1)}, s32[]{:S(2)}) async-start(s8[5767168]{0:T(1024)(128)(4,1)} %bitcast.66), calls=%async_computation.1 | async-start | bytes 8388608
  343.7 20.3 %copy-start.17 = (f32[2048]{0:T(1024)S(1)}, f32[2048]{0:T(1024)}, u32[]{:S(2)}) copy-start(f32[2048]{0:T(1024)} %copy-done.16) | copy-start | bytes 24580
  376.7 2.0 copy-start.1
  468.8 44.8 %copy-start.4 = (bf16[44,1024]{1,0:T(8,128)(2,1)S(1)}, bf16[44,1024]{1,0:T(8,128)(2,1)}, u32[]{:S(2)}) copy-start(bf16[44,1024]{1,0:T(8,128)(2,1)} %scatter_7.1) | copy-start | bytes 270340
  515.4 33.9 %copy-start.13 = (f32[2048]{0:T(1024)S(1)}, f32[2048]{0:T(1024)}, u32[]{:S(2)}) copy-start(f32[2048]{0:T(1024)} %copy-done.12) | copy-start | bytes 24580
  549.3 53.5 %copy-start.15 = (f32[2048]{0:T(1024)S(1)}, f32[2048]{0:T(1024)}, u32[]{:S(2)}) copy-start(f32[2048]{0:T(1024)} %copy-done.14) | copy-start | bytes 24580
  602.8 53.5 %copy-start.5 = (bf16[16,2816]{1,0:T(8,128)(2,1)S(1)}, bf16[16,2816]{1,0:T(8,128)(2,1)}, u32[]{:S(2)}) copy-start(bf16[16,2816]{1,0:T(8,128)(2,1)} %scatter_5.1) | copy-start | bytes 270340
  706.6 48.5 %copy-start.6 = (bf16[16,2816]{1,0:T(8,128)(2,1)S(1)}, bf16[16,2816]{1,0:T(8,128)(2,1)}, u32[]{:S(2)}) copy-start(bf16[16,2816]{1,0:T(8,128)(2,1)} %scatter_4.1) | copy-start | bytes 270340
  778.2 19.2 %copy-start.11 = (f32[2048]{0:T(1024)S(1)}, f32[2048]{0:T(1024)}, u32[]{:S(2)}) copy-start(f32[2048]{0:T(1024)} %copy-done.10) | copy-start | bytes 24580
  778.2 19.2 %copy-start = (bf16[1,2048,1024]{1,2,0:T(8,128)(2,1)S(1)}, bf16[1,2048,1024]{1,2,0:T(8,128)(2,1)}, u32[]{:S(2)}) copy-start(bf16[1,2048,1024]{1,2,0:T(8,128)(2,1)} %copy.15) | copy-start | bytes 12582916
  778.2 19.2 %copy-start.2 = (bf16[2048,1024]{0,1:T(8,128)(2,1)S(1)}, bf16[2048,1024]{0,1:T(8,128)(2,1)}, u32[]{:S(2)}) copy-start(bf16[2048,1024]{0,1:T(8,128)(2,1)} %copy-done.1) | copy-start | bytes 12582916

commit v2 on v1

--- a/solution.py
+++ b/solution.py
@@ -101,9 +101,11 @@
                 self.start(p,14)
         def e6():
             for p in P3:
-                for k in range(15): self.wait_send(p,k)
                 for k in range(11,15): self.wait_recv(p,k)
         return [e0,e1,e2,e3,e4,e5,e6]
+    def finish(self):
+        for p in range(3):
+            for k in range(15): self.wait_send(p,k)
 
 f32=jnp.float32
 
@@ -234,29 +236,237 @@
             pltpu.make_async_copy(self.res,self.out,self.osem).wait()
         return [e0,e1,e2,e3,e4,e5,e6,e7]
 
+T, D, FF = 2048, 1024, 2816
+F = 256
+N_F = FF // F
+M = 512
+N_T = T // M
+NT = (((1,), (1,)), ((), ()))
+TN = (((0,), (0,)), ((), ()))
+GU0 = (((0, 256), (256, 256), (512, 256)), ((768, 384), (1152, 384), (1536, 256)), ((1792, 384), (2176, 384), (2560, 256)))
+DD = ((0, 384), (384, 384), (768, 256))
+GU1 = (((0, 512), (512, 512), (1024, 384)), ((1408, 512), (1920, 512), (2432, 384)))
+HBM = pl.BlockSpec(memory_space=pltpu.HBM)
+VMEM = pl.BlockSpec(memory_space=pltpu.VMEM)
+
+
+def dot(a, b, dims=None):
+    if dims is None:
+        return jnp.dot(a, b, preferred_element_type=f32)
+    return lax.dot_general(a, b, dims, preferred_element_type=f32)
+
+
+def norm_rows(h):
+    wide = h.astype(f32)
+    return (wide * lax.rsqrt(jnp.mean(wide * wide, -1, keepdims=True) + 1e-6)).astype(bf)
+
+
+def run(events):
+    for event in events:
+        event()
+
+
+def at_step(i, events):
+    for step, functions in events.items():
+        pl.when(i == step)(functools.partial(run, functions))
+
+
+def tile(ref, f):
+    return ref.at[:, pl.ds(pl.multiple_of(f * F, F), F)]
+
+
+def forward_kernel(
+    x_hbm, dy_hbm, own0, own_d, own1,
+    gu0, dd, gu1, gate0, up0, act0, a0, h1, a1, act1, dgate1, dup1,
+    x, a, big, wt, go, raw, wc, ho, dyt, eo,
+    ssem, rsem, csem, xsem, wsem, gsem, bsem, rawsem, hsem, asem, dsem, esem,
+):
+    me = coords()
+    barrier(me)
+
+    def stream(k, own, out, cols):
+        g = Gather(me, own, out, ssem.at[k], rsem.at[k], csem.at[k], cols)
+        return g, g.events()
+
+    (gA, A), (gB, B), (gC, C) = (stream(k, own0, gu0, cols) for k, cols in enumerate(GU0))
+    gD, Dd = stream(3, own_d, dd, DD)
+    (gE, E), (gG, G) = (stream(4 + k, own1, gu1, cols) for k, cols in enumerate(GU1))
+
+    load_x = pltpu.make_async_copy(x_hbm, x, xsem.at[0])
+    load_x.start()
+    run([A[0], B[0]])
+    load_x.wait()
+
+    def norm0(t, _):
+        rows = pl.ds(pl.multiple_of(t * M, M), M)
+        a[rows, :] = norm_rows(x[rows, :])
+        return 0
+
+    lax.fori_loop(0, N_T, norm0, 0)
+    keep_a0 = pltpu.make_async_copy(a, a0, xsem.at[1])
+    keep_a0.start()
+    run([A[1], B[1], C[0], A[2], B[2], A[3], C[1], A[4], B[3], C[2], A[5], A[6], B[4], C[3]])
+
+    def load_w(w, f, slot):
+        return pltpu.make_async_copy(w.at[:, :, :, :, :, pl.ds(pl.multiple_of(f * F, F), F)], wt.at[slot], wsem.at[slot])
+
+    def put(f, slot):
+        return (
+            pltpu.make_async_copy(go.at[slot, 0], tile(gate0, f), gsem.at[slot, 0]),
+            pltpu.make_async_copy(go.at[slot, 1], tile(up0, f), gsem.at[slot, 1]),
+            pltpu.make_async_copy(tile(big, f), tile(act0, f), bsem.at[slot]),
+        )
+
+    def gate_up(f, events, w, finish):
+        slot = lax.rem(f, 2)
+        load_w(w, f, slot).wait()
+
+        @pl.when(f + 1 < N_F)
+        def _():
+            load_w(w, f + 1, 1 - slot).start()
+
+        finish(f, slot, [wt[slot, k].reshape(D, F) for k in (0, 1)])
+        at_step(f, events)
+        return 0
+
+    def finish0(f, slot, w):
+        @pl.when(f >= 2)
+        def _():
+            for copy in put(f - 2, slot):
+                copy.wait()
+
+        for t in range(N_T):
+            rows = pl.ds(t * M, M)
+            gate, up = dot(a[rows, :], w[0]), dot(a[rows, :], w[1])
+            go[slot, 0, rows, :] = gate
+            go[slot, 1, rows, :] = up
+            tile(big, f)[rows, :] = (gate * jax.nn.sigmoid(gate) * up).astype(bf)
+        for copy in put(f, slot):
+            copy.start()
+
+    ev = {
+        0: [B[5]], 1: [B[6], C[4]], 2: [C[5], Dd[0]], 3: [Dd[1]], 4: [Dd[2]], 5: [C[6], Dd[3]],
+        9: [Dd[4]], 10: [E[0], G[0]],
+    }
+    load_w(gu0, 0, 0).start()
+    lax.fori_loop(0, N_F, lambda f, _: gate_up(f, ev, gu0, finish0), 0)
+    run([Dd[5], E[1], Dd[6], G[1]])
+    load_raw = [pltpu.make_async_copy(dd.at[k], raw, rawsem) for k in (0, 1)]
+    load_raw[0].start()
+    for f in (N_F - 2, N_F - 1):
+        for copy in put(f, f % 2):
+            copy.wait()
+    keep_a0.wait()
+
+    def convert():
+        for i in range(64):
+            wc[44 * i : 44 * i + 44, :] = raw[i // 16, i // 4 % 4, i % 4]
+
+    load_raw[0].wait()
+    convert()
+    load_raw[1].start()
+
+    def put_h(t, slot):
+        return pltpu.make_async_copy(ho.at[slot], h1.at[pl.ds(pl.multiple_of(t * M, M), M)], hsem.at[slot])
+
+    def load_dy(t, slot):
+        return pltpu.make_async_copy(dy_hbm.at[pl.ds(pl.multiple_of(t * M, M), M)], dyt.at[slot], dsem.at[slot])
+
+    def down(t, events):
+        slot = lax.rem(t, 2)
+
+        @pl.when(t >= 2)
+        def _():
+            put_h(t - 2, slot).wait()
+
+        rows = pl.ds(pl.multiple_of(t * M, M), M)
+        h = (x[rows, :].astype(f32) + dot(big[rows, :], wc[...]).astype(bf).astype(f32)).astype(bf)
+        ho[slot] = h
+        a[rows, :] = norm_rows(h)
+        put_h(t, slot).start()
+        at_step(t, events)
+        return 0
+
+    lax.fori_loop(0, N_T, lambda t, _: down(t, {0: [E[2]], 1: [G[2], E[3]]}), 0)
+    keep_a1 = pltpu.make_async_copy(a, a1, asem)
+    keep_a1.start()
+    load_dy(0, 0).start()
+    for t in (N_T - 2, N_T - 1):
+        put_h(t, t % 2).wait()
+    load_raw[1].wait()
+    convert()
+
+    def dact(t, events):
+        slot = lax.rem(t, 2)
+        load_dy(t, slot).wait()
+
+        @pl.when(t + 1 < N_T)
+        def _():
+            load_dy(t + 1, 1 - slot).start()
+
+        rows = pl.ds(pl.multiple_of(t * M, M), M)
+        big[rows, :] = dot(dyt[slot], wc[...], NT).astype(bf)
+        at_step(t, events)
+        return 0
+
+    lax.fori_loop(0, N_T, lambda t, _: dact(t, {0: [E[4], G[3]], 2: [E[5]], 3: [E[6], G[4]]}), 0)
+
+    def put1(f, slot):
+        return [pltpu.make_async_copy(eo.at[slot, k], tile(out, f), esem.at[slot, k]) for k, out in enumerate((act1, dgate1, dup1))]
+
+    def finish1(f, slot, w):
+        @pl.when(f >= 2)
+        def _():
+            for copy in put1(f - 2, slot):
+                copy.wait()
+
+        for t in range(N_T):
+            rows = pl.ds(t * M, M)
+            gate, up = dot(a[rows, :], w[0]), dot(a[rows, :], w[1])
+            by_act = tile(big, f)[rows, :].astype(f32)
+            sig = jax.nn.sigmoid(gate)
+            silu = gate * sig
+            eo[slot, 0, rows, :] = (silu * up).astype(bf)
+            eo[slot, 1, rows, :] = (by_act * up * (sig + silu * (1 - sig))).astype(bf)
+            eo[slot, 2, rows, :] = (by_act * silu).astype(bf)
+        for copy in put1(f, slot):
+            copy.start()
+
+    load_w(gu1, 0, 0).start()
+    lax.fori_loop(0, N_F, lambda f, _: gate_up(f, {1: [G[5]], 2: [G[6]]}, gu1, finish1), 0)
+    for f in (N_F - 2, N_F - 1):
+        for copy in put1(f, f % 2):
+            copy.wait()
+    keep_a1.wait()
+    for g in (gA, gB, gC, gD, gE, gG):
+        g.finish()
+
+
+def forward(x, dy, own0, own_d, own1):
+    sd = jax.ShapeDtypeStruct
+    wide, wide32, narrow = sd((T, FF), bf), sd((T, FF), f32), sd((T, D), bf)
+    dma = pltpu.SemaphoreType.DMA
+    return pl.pallas_call(
+        forward_kernel,
+        in_specs=[HBM, HBM, VMEM, VMEM, VMEM],
+        out_specs=[HBM] * 12,
+        out_shape=[sd((2, 4, 4, 4, 16, FF), bf), sd((2, 4, 4, 4, 44, D), bf), sd((2, 4, 4, 4, 16, FF), bf),
+                   wide32, wide32, wide, narrow, narrow, narrow, wide, wide, wide],
+        scratch_shapes=[
+            pltpu.VMEM((T, D), bf), pltpu.VMEM((T, D), bf), pltpu.VMEM((T, FF), bf),
+            pltpu.VMEM((2, 2, 4, 4, 4, 16, F), bf), pltpu.VMEM((2, 2, T, F), f32),
+            pltpu.VMEM((4, 4, 4, 44, D), bf), pltpu.VMEM((FF, D), bf), pltpu.VMEM((2, M, D), bf),
+            pltpu.VMEM((2, M, D), bf), pltpu.VMEM((2, 3, T, F), bf),
+            dma((6, 3, 15)), dma((6, 3, 15)), dma((6, 3)), dma((2,)), dma((2,)), dma((2, 2)), dma((2,)), dma(()), dma((2,)), dma(()), dma((2,)), dma((2, 3)),
+        ],
+        compiler_params=pltpu.CompilerParams(collective_id=0, has_side_effects=True, vmem_limit_bytes=63 * 2**20),
+        name="forward",
+    )(x, dy, own0, own_d, own1)
+
+
 NAMES = ("w_gate", "w_up", "w_down")
 GU_COLS = ((0, 1024), (1024, 896), (1920, 896))
 D_COLS = ((0, 384), (384, 384), (768, 256))
-
-
-def gather_call(pair, cols, number):
-    rows, width = pair.shape[1:]
-
-    def kernel(own, out, *sems):
-        me = coords()
-        barrier(me)
-        for event in Gather(me, own, out, *sems, cols).events():
-            event()
-
-    return pl.pallas_call(
-        kernel,
-        in_specs=[pl.BlockSpec(memory_space=pltpu.VMEM)],
-        out_specs=pl.BlockSpec(memory_space=pltpu.HBM),
-        out_shape=jax.ShapeDtypeStruct((2, 4, 4, 4, rows, width), bf),
-        scratch_shapes=[pltpu.SemaphoreType.DMA((3, 15)), pltpu.SemaphoreType.DMA((3, 15)), pltpu.SemaphoreType.DMA((3,))],
-        compiler_params=pltpu.CompilerParams(collective_id=number, has_side_effects=True),
-        name=f"gather_{number}",
-    )(pair)
 
 
 def scatter_call(g, cols, number):
@@ -279,40 +489,43 @@
     )(g)
 
 
-def matmul(a, w):
-    return jnp.dot(a, w, preferred_element_type=f32).astype(bf)
-
-
-def normed(h):
+def mm(a, w, dims):
+    return lax.dot_general(a, w, dims, preferred_element_type=f32).astype(bf)
+
+
+def norm_back(h, by_a, by_h):
     wide = h.astype(f32)
     scale = lax.rsqrt(jnp.mean(wide**2, -1, keepdims=True) + 1e-6)
-    return (wide * scale).astype(bf)
-
-
-def layer(h, w):
-    a = normed(h)
-    gate = jnp.dot(a, w["w_gate"], preferred_element_type=f32)
-    up = jnp.dot(a, w["w_up"], preferred_element_type=f32)
-    return h + matmul((jax.nn.silu(gate) * up).astype(bf), w["w_down"])
-
-
-def stack(weights, h):
-    for w in weights:
-        h = layer(h, w)
-    return h
+    by_a = by_a.astype(f32)
+    by_wide = scale * by_a - wide * (scale**3 * jnp.mean(wide * by_a, -1, keepdims=True))
+    return (by_h.astype(f32) + by_wide.astype(bf).astype(f32)).astype(bf)
 
 
 def solution(mesh):
     def device(x, dy, w_gate, w_up, w_down):
-        gu = [gather_call(jnp.stack([w_gate[n], w_up[n]]), GU_COLS, n).reshape(2, 1024, 2816) for n in (0, 1)]
-        dd = gather_call(w_down, D_COLS, 2).reshape(2, 2816, 1024)
-        weights = [dict(zip(NAMES, (*gu[n], dd[n]), strict=True)) for n in (0, 1)]
-        _, back = jax.vjp(stack, weights, x[0])
-        by_weights, by_x = back(dy[0])
+        x, dy = x[0], dy[0]
+        own0, own1 = (jnp.stack([w_gate[n], w_up[n]]) for n in (0, 1))
+        gu0, dd, gu1, gate0, up0, act0, a0, h1, a1, act1, dgate1, dup1 = forward(x, dy, own0, w_down, own1)
+        gu0, gu1 = (t.reshape(2, D, FF) for t in (gu0, gu1))
+        dd = dd.reshape(2, FF, D)
+        by = {}
+        by["w_down", 1] = mm(act1, dy, TN)
+        by["w_gate", 1] = mm(a1, dgate1, TN)
+        by["w_up", 1] = mm(a1, dup1, TN)
+        dh = norm_back(h1, mm(dgate1, gu1[0], NT) + mm(dup1, gu1[1], NT), dy)
+        by["w_down", 0] = mm(act0, dh, TN)
+        ds = mm(dh, dd[0], NT).astype(f32)
+        sig = jax.nn.sigmoid(gate0)
+        silu = gate0 * sig
+        dgate0 = (ds * up0 * (sig + silu * (1 - sig))).astype(bf)
+        dup0 = (ds * silu).astype(bf)
+        by["w_gate", 0] = mm(a0, dgate0, TN)
+        by["w_up", 0] = mm(a0, dup0, TN)
+        by_x = norm_back(x, mm(dgate0, gu0[0], NT) + mm(dup0, gu0[1], NT), dh)
         outs = []
         for j, name in enumerate(NAMES):
             rows, cols = (44, D_COLS) if name == "w_down" else (16, GU_COLS)
-            both = [scatter_call(by_weights[n][name].reshape(4, 4, 4, rows, -1), cols, 3 + 2 * j + n) for n in (0, 1)]
+            both = [scatter_call(by[name, n].reshape(4, 4, 4, rows, -1), cols, 3 + 2 * j + n) for n in (0, 1)]
             outs.append(jnp.stack(both))
         return (by_x[None], *outs)
 

time: 819 us -> 649 us (0.79)
  matrix products: 377 us -> 212 us
  local copies, waits for them, and re-layouts: 90.5 us -> 58.3 us
  Pallas kernels: 322 us -> 351 us
    dot_general x17 -> x11, matrix products: 377 us -> 212 us  [mm(): return lax.dot_general(a, w, dims, preferred_element_type=f32).astype(bf)]
    pallas_call x3 -> x1, Pallas kernels: 124 us -> 153 us  [forward(): pl.pallas_call(forward_kernel, in_specs=[HBM, HBM, VMEM, VMEM, VMEM], out...]
    unnamed x45 -> x26, local copies, waits for them, and re-layouts: 23 us -> 2.54 us
    another operation x2 -> x0, local copies, waits for them, and re-layouts: 19.5 us -> none  [device(): weights = [dict(zip(NAMES, (*gu[n], dd[n]), strict=True)) for n in (0, 1)]]
    slice x3 -> x5, local copies, waits for them, and re-layouts: 11.2 us -> 28.4 us  [the longest x1 9.94 us: device(): by_x = norm_back(x, mm(dgate0, gu0[0], NT) + mm(dup0, gu0[1], NT), dh)]
    squeeze x2 -> x1, local copies, waits for them, and re-layouts: 18.3 us -> 9.11 us  [device(): ds = mm(dh, dd[0], NT).astype(f32)]
where the time goes in v2:
time: 649 us; the launch traced here: 639 us
  Pallas kernels  351 us (54%)
  matrix products  212 us (33%)
  local copies, waits for them, and re-layouts  58.3 us (9%)
  other arithmetic  17.3 us (3%)
    dot_general x11, matrix products, mm(): return lax.dot_general(a, w, dims, preferred_element_type=f32).astype(bf)  212 us
    pallas_call x6, Pallas kernels, scatter_call(): pl.pallas_call(kernel, in_specs=[pl.BlockSpec(memory_space=pltpu.HBM)], o...  198 us
    pallas_call x1, Pallas kernels, forward(): pl.pallas_call(forward_kernel, in_specs=[HBM, HBM, VMEM, VMEM, VMEM], out...  153 us
    reshape x2, local copies, waits for them, and re-layouts, device(): by[name, n].reshape(4, 4, 4, rows, -1)  18.2 us

profile of v2, /device:TPU:0, one launch (start us, length us, event | category | flops | bytes accessed | tf_op | source)
XLA Modules:
  0.0 639.2 jit_solution(2729763550903741099)
XLA Ops:
  0.6 0.9 fusion.18
  1.6 0.9 fusion.19
  2.5 0.8 pad_maximum_fusion.1
  3.3 1.6 copy.15.own_d
  4.9 153.0 %forward.1 = (bf16[2,4,4,4,16,2816]{5,4,3,2,1,0:T(8,128)(2,1)}, bf16[2,4,4,4,44,1024]{5,4,3,2,1,0:T(8,128)(2,1)}, bf16[2,4,4,4,16,2816]{5,4,3,2,1,0:T(8,128)(2,1...) custom-call(bf16[2048,1024]{1,0:T(8,128)(2,1)} %bitcast.46, ...), custom_call_target="tpu_custom_call" | custom-call | tf_op jit(solution)/shard_map/forward/pallas_call | solution.py:449
  157.9 9.8 %fusion.17 = (bf16[1,4,4,4,16,2816]{5,4,3,2,1,0:T(8,128)(2,1)}, bf16[1,4,4,4,16,2816]{5,4,3,2,1,0:T(8,128)(2,1)}) fusion(bf16[2,4,4,4,16,2816]{5,4,3,2,1,0:T(8,128)(2,1)} %get-tuple-element.18), kind=kLoop, calls=%fused_computation.48 | loop fusion | bytes 23068672 | tf_op jit(solution)/shard_map/slice | solution.py:515
  167.7 17.6 %fusion.20 = bf16[2048,1024]{1,0:T(8,128)(2,1)} fusion(bf16[2048,2816]{1,0:T(8,128)(2,1)} %get-tuple-element.17, bf16[1024,2816]{1,0:T(8,128)(2,1)} %bitcast.54), kind=kOutput, calls=%fused_computation.51 | convolution fusion | flops 11811160064 | bytes 21495808 | tf_op jit(solution)/shard_map/dot_general | solution.py:493
  185.4 0.0 copy-done.7
  185.4 0.0 copy-done.8
  185.4 14.1 %convolution_convert_fusion.5 = bf16[1024,2816]{1,0:T(8,128)(2,1)} fusion(bf16[2048,1024]{1,0:T(8,128)(2,1)S(1)} %copy-done.8, bf16[2048,2816]{1,0:T(8,128)(2,1)S(1)} %copy-done.7), kind=kOutput, calls=%fused_computation.30 | convolution fusion | flops 11814043648 | bytes 21495808 | tf_op jit(solution)/shard_map/dot_general | solution.py:493
  199.5 0.0 copy-done.3
  199.5 18.2 %fusion.8 = (f32[2048]{0:T(1024)S(1)}, f32[2048]{0:T(1024)S(1)}, bf16[2048,1024]{1,0:T(8,128)(2,1)}) fusion(bf16[2048,1024]{1,0:T(8,128)(2,1)} %get-tuple-element.16, bf16[2048,1024]{1,0:T(8,128)(2,1)} %fusion.20, bf16[2048,2816]{1,0:T(8,128)(2,1)} %get-tuple-element.19, bf16[1024,2816]{1,0:T(8,128)(2,1)S(1)} %bitcast.51), kind=kOutput, calls=%fused_computation.20 | convolution fusion | flops 11827933184 | bytes 29900800 | tf_op jit(solution)/shard_map/dot_general | solution.py:493
  217.6 19.1 %convolution_convert_fusion.3 = bf16[1024,2816]{1,0:T(8,128)(2,1)} fusion(bf16[2048,1024]{1,0:T(8,128)(2,1)} %get-tuple-element.25, bf16[2048,2816]{1,0:T(8,128)(2,1)} %get-tuple-element.19), kind=kOutput, calls=%fused_computation.28 | convolution fusion | flops 11814043648 | bytes 21495808 | tf_op jit(solution)/shard_map/dot_general | solution.py:493
  236.8 37.9 %scatter_6.1 = bf16[16,2816]{1,0:T(8,128)(2,1)} custom-call(bf16[4,4,4,16,2816]{4,3,2,1,0:T(8,128)(2,1)} %bitcast.48), custom_call_target="tpu_custom_call" | custom-call | tf_op jit(solution)/shard_map/scatter_6/pallas_call | solution.py:481
  274.7 33.3 %scatter_4.1 = bf16[16,2816]{1,0:T(8,128)(2,1)} custom-call(bf16[4,4,4,16,2816]{4,3,2,1,0:T(8,128)(2,1)} %bitcast.47), custom_call_target="tpu_custom_call" | custom-call | tf_op jit(solution)/shard_map/scatter_4/pallas_call | solution.py:481
  308.0 0.0 copy-start.2
  308.0 0.0 slice-start
  308.0 6.5 %add_convert_fusion.1 = bf16[2048,1024]{1,0:T(8,128)(2,1)S(1)} fusion(bf16[2048,1024]{1,0:T(8,128)(2,1)} %get-tuple-element.16, bf16[2048,1024]{1,0:T(8,128)(2,1)} %get-tuple-element.54, f32[2048]{0:T(1024)S(1)} %get-tuple-element.53, f32[2048]{0:T(1024)S(1)} %get-tuple-element.52, bf16[1,2048,1024]{2,1,0:T(8,128)(2,1)} %param.6), kind=kLoop, calls=%fused_computation.25 | loop fusion | flops 20971520 | bytes 16793600 | tf_op jit(solution)/shard_map/convert_element_type | solution.py:501
  314.5 0.0 copy-done.2
  314.5 0.0 copy-start
  314.5 0.0 slice-start.1
  314.5 0.0 slice-start.2
  314.5 18.8 %convolution_convert_fusion.1 = bf16[2816,1024]{1,0:T(8,128)(2,1)} fusion(bf16[2048,2816]{1,0:T(8,128)(2,1)} %get-tuple-element.27, bf16[1,2048,1024]{2,1,0:T(8,128)(2,1)S(1)} %copy-done.2), kind=kOutput, calls=%fused_computation.26 | convolution fusion | flops 11814043648 | bytes 21495808 | tf_op jit(solution)/shard_map/dot_general | solution.py:493
  333.3 0.0 copy-done
  333.3 0.0 slice-done
  333.3 0.0 slice-done.1
  333.3 0.0 slice-done.2
  333.3 14.1 %convolution_convert_fusion.2 = bf16[2816,1024]{1,0:T(8,128)(2,1)} fusion(bf16[2048,2816]{1,0:T(8,128)(2,1)S(1)} %bitcast.62, bf16[2048,1024]{1,0:T(8,128)(2,1)S(1)} %add_convert_fusion.1), kind=kOutput, calls=%fused_computation.27 | convolution fusion | flops 11814043648 | bytes 21495808 | tf_op jit(solution)/shard_map/dot_general | solution.py:493
  347.5 9.1 %reshape.83.g = bf16[4,4,4,44,1024]{4,3,2,1,0:T(8,128)(2,1)} reshape(bf16[2816,1024]{1,0:T(8,128)(2,1)} %convolution_convert_fusion.2) | data formatting | bytes 11534336 | tf_op jit(solution)/shard_map/reshape | solution.py:528
  356.6 34.8 %scatter_7.1 = bf16[44,1024]{1,0:T(8,128)(2,1)} custom-call(bf16[4,4,4,44,1024]{4,3,2,1,0:T(8,128)(2,1)} %reshape.83.g), custom_call_target="tpu_custom_call" | custom-call | tf_op jit(solution)/shard_map/scatter_7/pallas_call | solution.py:481
  391.3 9.1 %reshape.84.g = bf16[4,4,4,44,1024]{4,3,2,1,0:T(8,128)(2,1)} reshape(bf16[2816,1024]{1,0:T(8,128)(2,1)} %convolution_convert_fusion.1) | data formatting | bytes 11534336 | tf_op jit(solution)/shard_map/reshape | solution.py:528
  400.5 32.2 %scatter_8.1 = bf16[44,1024]{1,0:T(8,128)(2,1)} custom-call(bf16[4,4,4,44,1024]{4,3,2,1,0:T(8,128)(2,1)} %reshape.84.g), custom_call_target="tpu_custom_call" | custom-call | tf_op jit(solution)/shard_map/scatter_8/pallas_call | solution.py:481
  432.7 0.0 copy-done.4
  432.7 0.9 pad_maximum_fusion
  433.6 0.9 copy.20
  434.5 6.8 %slice.38 = bf16[1,4,4,4,44,1024]{5,4,3,2,1,0:T(8,128)(2,1)} slice(bf16[2,4,4,4,44,1024]{5,4,3,2,1,0:T(8,128)(2,1)} %get-tuple-element.20), slice={[0:1], [0:4], [0:4], [0:4], [0:44], [0:1024]} | slice | bytes 11534336 | tf_op jit(solution)/shard_map/slice | solution.py:517
  441.3 9.1 %squeeze.25 = bf16[2816,1024]{1,0:T(8,128)(2,1)} reshape(bf16[1,4,4,4,44,1024]{5,4,3,2,1,0:T(8,128)(2,1)} %slice.38) | data formatting | bytes 11534336 | tf_op jit(solution)/shard_map/squeeze | solution.py:517
  450.4 32.6 %fusion.2 = (bf16[2048,2816]{1,0:T(8,128)(2,1)}, bf16[2048,2816]{1,0:T(8,128)(2,1)}) fusion(f32[2048,2816]{1,0:T(8,128)} %get-tuple-element.22, f32[2048,2816]{1,0:T(8,128)} %get-tuple-element.21, bf16[2048,1024]{1,0:T(8,128)(2,1)} %copy-done, bf16[2816,1024]{1,0:T(8,128)(2,1)} %squeeze.25), kind=kOutput, calls=%fused_computation.4 | convolution fusion | flops 11891900416 | bytes 79167488 | tf_op jit(solution)/shard_map/dot_general | solution.py:493
  483.0 19.2 %convolution_convert_fusion.4 = bf16[1024,2816]{1,0:T(8,128)(2,1)} fusion(bf16[2048,1024]{1,0:T(8,128)(2,1)} %get-tuple-element.24, bf16[2048,2816]{1,0:T(8,128)(2,1)} %get-tuple-element.40), kind=kOutput, calls=%fused_computation.29 | convolution fusion | flops 11814043648 | bytes 21495808 | tf_op jit(solution)/shard_map/dot_general | solution.py:493
  502.2 29.9 %scatter_5.1 = bf16[16,2816]{1,0:T(8,128)(2,1)} custom-call(bf16[4,4,4,16,2816]{4,3,2,1,0:T(8,128)(2,1)} %bitcast.50), custom_call_target="tpu_custom_call" | custom-call | tf_op jit(solution)/shard_map/scatter_5/pallas_call | solution.py:481
  532.1 1.6 pad_maximum_fusion.4
  533.7 19.0 %convolution_convert_fusion.6 = bf16[1024,2816]{1,0:T(8,128)(2,1)} fusion(bf16[2048,1024]{1,0:T(8,128)(2,1)} %get-tuple-element.24, bf16[2048,2816]{1,0:T(8,128)(2,1)} %get-tuple-element.41), kind=kOutput, calls=%fused_computation.31 | convolution fusion | flops 11814043648 | bytes 21495808 | tf_op jit(solution)/shard_map/dot_general | solution.py:493
  552.7 29.7 %scatter_3.1 = bf16[16,2816]{1,0:T(8,128)(2,1)} custom-call(bf16[4,4,4,16,2816]{4,3,2,1,0:T(8,128)(2,1)} %bitcast.49), custom_call_target="tpu_custom_call" | custom-call | tf_op jit(solution)/shard_map/scatter_3/pallas_call | solution.py:481
  582.5 1.6 pad_maximum_fusion.3
  584.0 9.9 %fusion.16 = (bf16[1,4,4,4,16,2816]{5,4,3,2,1,0:T(8,128)(2,1)}, bf16[1,4,4,4,16,2816]{5,4,3,2,1,0:T(8,128)(2,1)}) fusion(bf16[2,4,4,4,16,2816]{5,4,3,2,1,0:T(8,128)(2,1)} %get-tuple-element.23), kind=kLoop, calls=%fused_computation.47 | loop fusion | bytes 23068672 | tf_op jit(solution)/shard_map/slice | solution.py:524
  594.0 17.5 %fusion.21 = bf16[2048,1024]{1,0:T(8,128)(2,1)} fusion(bf16[2048,2816]{1,0:T(8,128)(2,1)} %get-tuple-element.41, bf16[1024,2816]{1,0:T(8,128)(2,1)} %bitcast.53), kind=kOutput, calls=%fused_computation.52 | convolution fusion | flops 11811160064 | bytes 21495808 | tf_op jit(solution)/shard_map/dot_general | solution.py:493
  611.5 21.4 %fusion.10 = (f32[2048]{0:T(1024)S(1)}, f32[2048]{0:T(1024)S(1)}, bf16[2048,1024]{1,0:T(8,128)(2,1)}) fusion(bf16[1,2048,1024]{2,1,0:T(8,128)(2,1)} %param.5, bf16[2048,1024]{1,0:T(8,128)(2,1)} %fusion.21, bf16[2048,2816]{1,0:T(8,128)(2,1)} %get-tuple-element.40, bf16[1024,2816]{1,0:T(8,128)(2,1)} %bitcast.52), kind=kOutput, calls=%fused_computation.22 | convolution fusion | flops 11827933184 | bytes 29900800 | tf_op jit(solution)/shard_map/dot_general | solution.py:493
  632.8 5.9 fusion.12
  (13 shorter events, 0.0 us)
Async XLA Ops:
  167.7 17.6 %copy-start.7 = (bf16[2048,2816]{1,0:T(8,128)(2,1)S(1)}, bf16[2048,2816]{1,0:T(8,128)(2,1)}, u32[]{:S(2)}) copy-start(bf16[2048,2816]{1,0:T(8,128)(2,1)} %get-tuple-element.17) | copy-start | bytes 34603012
  167.7 17.6 %copy-start.8 = (bf16[2048,1024]{1,0:T(8,128)(2,1)S(1)}, bf16[2048,1024]{1,0:T(8,128)(2,1)}, u32[]{:S(2)}) copy-start(bf16[2048,1024]{1,0:T(8,128)(2,1)} %get-tuple-element.25) | copy-start | bytes 12582916
  185.4 14.1 %copy-start.3 = (bf16[1,4,4,4,16,2816]{5,4,3,2,1,0:T(8,128)(2,1)S(1)}, bf16[1,4,4,4,16,2816]{5,4,3,2,1,0:T(8,128)(2,1)}, u32[]{:S(2)}) copy-start(bf16[1,4,4,4,16,2816]{5,4,3,2,1,0:T(8,128)(2,1)} %get-tuple-element.44) | copy-start | bytes 17301508
  308.0 6.5 %copy-start.2 = (bf16[1,2048,1024]{2,1,0:T(8,128)(2,1)S(1)}, bf16[1,2048,1024]{2,1,0:T(8,128)(2,1)}, u32[]{:S(2)}) copy-start(bf16[1,2048,1024]{2,1,0:T(8,128)(2,1)} %param.6) | copy-start | bytes 12582916
  308.0 25.3 %slice-start = ((s8[11534336]{0:T(1024)(128)(4,1)}), s8[4194304]{0:T(1024)(128)(4,1)S(1)}, s32[]{:S(2)}) async-start(s8[11534336]{0:T(1024)(128)(4,1)} %bitcast.61), calls=%async_computation | async-start | bytes 8388608
  314.5 18.8 %copy-start = (bf16[2048,1024]{1,0:T(8,128)(2,1)}, bf16[2048,1024]{1,0:T(8,128)(2,1)S(1)}, u32[]{:S(2)}) copy-start(bf16[2048,1024]{1,0:T(8,128)(2,1)S(1)} %add_convert_fusion.1) | copy-start | bytes 12582916
  314.5 18.8 %slice-start.1 = ((s8[11534336]{0:T(1024)(128)(4,1)}), s8[4194304]{0:T(1024)(128)(4,1)S(1)}, s32[]{:S(2)}) async-start(s8[11534336]{0:T(1024)(128)(4,1)} %bitcast.61), calls=%async_computation.1 | async-start | bytes 8388608
  314.5 18.8 %slice-start.2 = ((s8[11534336]{0:T(1024)(128)(4,1)}), s8[3145728]{0:T(1024)(128)(4,1)S(1)}, s32[]{:S(2)}) async-start(s8[11534336]{0:T(1024)(128)(4,1)} %bitcast.61), calls=%async_computation.2 | async-start | bytes 6291456
  391.3 41.4 %copy-start.4 = (bf16[44,1024]{1,0:T(8,128)(2,1)S(1)}, bf16[44,1024]{1,0:T(8,128)(2,1)}, u32[]{:S(2)}) copy-start(bf16[44,1024]{1,0:T(8,128)(2,1)} %scatter_7.1) | copy-start | bytes 270340
  483.0 49.1 %copy-start.6 = (bf16[16,2816]{1,0:T(8,128)(2,1)S(1)}, bf16[16,2816]{1,0:T(8,128)(2,1)}, u32[]{:S(2)}) copy-start(bf16[16,2816]{1,0:T(8,128)(2,1)} %scatter_6.1) | copy-start | bytes 270340
  533.7 48.8 %copy-start.5 = (bf16[16,2816]{1,0:T(8,128)(2,1)S(1)}, bf16[16,2816]{1,0:T(8,128)(2,1)}, u32[]{:S(2)}) copy-start(bf16[16,2816]{1,0:T(8,128)(2,1)} %scatter_4.1) | copy-start | bytes 270340
  611.5 21.4 %copy-start.1 = (bf16[2048,1024]{1,0:T(8,128)(2,1)S(1)}, bf16[2048,1024]{1,0:T(8,128)(2,1)}, u32[]{:S(2)}) copy-start(bf16[2048,1024]{1,0:T(8,128)(2,1)} %copy-done) | copy-start | bytes 12582916

commit v3 on v0

v3 whole, which is shorter than its diff:
```python
import functools
import jax, jax.numpy as jnp
from jax import lax
from jax.experimental import pallas as pl
from jax.experimental.pallas import tpu as pltpu
from jax.sharding import PartitionSpec as P
ZERO, ONE, TWO, THREE, FOUR, FIVE, SIX, SEVEN, EIGHT, NINE, TEN, ELEVEN, TWELVE = range(13)
ROWS = 1024 // 64
bf=jnp.bfloat16
MESH=pl.DeviceIdType.MESH
PERM=((ZERO,ONE,TWO),(ONE,TWO,ZERO),(TWO,ZERO,ONE))

class Place:
    def __init__(self):
        i=lax.axis_index("dp")
        self.plus=[[c,*((c+d)%FOUR for d in range(ONE,FOUR))] for c in (i//ROWS,(i//FOUR)%FOUR,i%FOUR)]
        self.near=[]
        for a in range(THREE):
            c=[self.plus[b][ZERO] for b in range(THREE)]
            self.near.append([{"dp":(c[:a]+[self.plus[a][d]]+c[a+ONE:])[ZERO]*ROWS+(c[:a]+[self.plus[a][d]]+c[a+ONE:])[ONE]*FOUR+(c[:a]+[self.plus[a][d]]+c[a+ONE:])[TWO]} for d in range(FOUR)])

def coords():
    return Place()

def shifted(me,axis,d):
    return me.near[axis][d]

def peers(me,far=True):
    return [shifted(me,a,d) for a in range(THREE) for d in ((ONE,THREE,TWO) if far else (ONE,THREE))]

def barrier(me,far=True,sib=True):
    b=pltpu.get_barrier_semaphore()
    n=ZERO
    for t in peers(me,far):
        pl.semaphore_signal(b,inc=ONE,device_id=t,device_id_type=MESH); n+=ONE
    if sib:
        pl.semaphore_signal(b,inc=ONE,device_id={"rep":ONE-lax.axis_index("rep")},device_id_type=MESH); n+=ONE
    pl.semaphore_wait(b,n)

class Gather:
    NSEM=15
    def __init__(self,me,own,out,ssem,rsem,lsem,cols):
        self.me,self.own,self.out,self.ssem,self.rsem,self.lsem,self.cols=me,own,out,ssem,rsem,lsem,cols
        self.r=lax.axis_index("rep"); self.sib={"rep":ONE-self.r}
    def at(self,p,r,u,v,w):
        i=[None]*THREE
        for a,k in zip(PERM[p],(u,v,w)): i[a]=k
        return self.out.at[(r,pl.ds(*self.cols[p]),*i)]
    def copy(self,p,k,src,dst,dev):
        return pltpu.make_async_remote_copy(src_ref=src,dst_ref=dst,send_sem=self.ssem.at[p,k],recv_sem=self.rsem.at[p,k],device_id=dev,device_id_type=MESH)
    def m(self,p,k,d=ZERO): return self.me.plus[PERM[p][k]][d]
    def sent(self,p,k):
        r=self.r; u,v,w=(self.m(p,j) for j in range(THREE)); A=slice(None); lo,hi=pl.ds(ZERO,TWO),pl.ds(TWO,TWO)
        near=[self.me.near[a] for a in PERM[p]]
        if k<THREE: return self.own.at[r,pl.ds(*self.cols[p])],self.at(p,r,u,v,w),near[ZERO][(ONE,THREE,TWO)[k]]
        if k<FIVE: ref,to=self.at(p,r,A,v,w),near[ONE][(ONE,THREE)[k-THREE]]
        elif k<SEVEN: ref,to=self.at(p,r,(lo,hi)[k-FIVE],self.m(p,ONE,(THREE,ONE)[k-FIVE]),w),near[ONE][(ONE,THREE)[k-FIVE]]
        elif k<NINE: ref,to=self.at(p,r,A,A,w),near[TWO][(ONE,THREE)[k-SEVEN]]
        elif k<ELEVEN: ref,to=self.at(p,r,(lo,hi)[k-NINE],A,self.m(p,TWO,(THREE,ONE)[k-NINE])),near[TWO][(ONE,THREE)[k-NINE]]
        else: ref,to=self.at(p,r,A,A,self.m(p,TWO,(ZERO,THREE,ONE,TWO)[k-ELEVEN])),self.sib
        return ref,ref,to
    def received(self,p,k):
        r=self.r; v,w=self.m(p,ONE),self.m(p,TWO); A=slice(None); lo,hi=pl.ds(ZERO,TWO),pl.ds(TWO,TWO)
        if k<THREE: return self.at(p,r,self.m(p,ZERO,(THREE,ONE,TWO)[k]),v,w)
        if k<FIVE: return self.at(p,r,A,self.m(p,ONE,(THREE,ONE)[k-THREE]),w)
        if k<SEVEN: return self.at(p,r,(lo,hi)[k-FIVE],self.m(p,ONE,TWO),w)
        if k<NINE: return self.at(p,r,A,A,self.m(p,TWO,(THREE,ONE)[k-SEVEN]))
        if k<ELEVEN: return self.at(p,r,(lo,hi)[k-NINE],A,self.m(p,TWO,TWO))
        return self.at(p,ONE-r,A,A,self.m(p,TWO,(ZERO,THREE,ONE,TWO)[k-ELEVEN]))
    def start(self,p,k):
        s,d,dev=self.sent(p,k); self.copy(p,k,s,d,dev).start()
    def wait_send(self,p,k):
        s,d,dev=self.sent(p,k); self.copy(p,k,s,d,dev).wait_send()
    def wait_recv(self,p,k):
        ref=self.received(p,k); self.copy(p,k,ref,ref,self.sib).wait_recv()
    def local(self,p):
        return pltpu.make_async_copy(self.own.at[self.r,pl.ds(*self.cols[p])],self.at(p,self.r,*(self.m(p,j) for j in range(THREE))),self.lsem.at[p])
    def events(self):
        P3=range(THREE)
        def e0():
            for p in P3:
                self.local(p).start()
                for k in (ZERO,ONE,TWO): self.start(p,k)
        def e1():
            for p in P3:
                self.local(p).wait()
                for k in (ZERO,ONE,TWO): self.wait_recv(p,k)
                for k in (THREE,FOUR): self.start(p,k)
        def e2():
            for p in P3:
                for k in (THREE,FOUR): self.wait_recv(p,k); self.start(p,k+TWO)
        def e3():
            for p in P3:
                for k in (FIVE,SIX): self.wait_recv(p,k)
                for k in (SEVEN,EIGHT,ELEVEN): self.start(p,k)
        def e4():
            for p in P3:
                for k in (SEVEN,EIGHT): self.wait_recv(p,k); self.start(p,k+TWO); self.start(p,k+FIVE)
        def e5():
            for p in P3:
                for k in (NINE,TEN): self.wait_recv(p,k)
                self.start(p,14)
        def e6():
            for p in P3:
                for k in range(ELEVEN,15): self.wait_recv(p,k)
        return [e0,e1,e2,e3,e4,e5,e6]
    def finish(self):
        for p in range(THREE):
            for k in range(15): self.wait_send(p,k)

f32=jnp.float32

T, D, FF, LAYERS = 2048, 1024, 2816, TWO
F = 256
N_F = FF // F
M = 512
N_T = T // M
NT = (((ONE,), (ONE,)), ((), ()))
TN = (((ZERO,), (ZERO,)), ((), ()))
L = 128
C = FF // L
GU0 = (((ZERO, TWO), (TWO, TWO), (FOUR, TWO)), ((SIX, THREE), (NINE, THREE), (TWELVE, TWO)), ((14, THREE), (17, THREE), (20, TWO)))
DD = ((ZERO, FOUR), (FOUR, FOUR), (EIGHT, THREE))
GU1 = (((ZERO, FOUR), (FOUR, THREE), (SEVEN, FOUR)), ((ELEVEN, THREE), (14, FOUR), (18, FOUR)))
HBM = pl.BlockSpec(memory_space=pltpu.HBM)
VMEM = pl.BlockSpec(memory_space=pltpu.VMEM)


def dot(a, b, dims=None):
    if dims is None:
        return jnp.dot(a, b, preferred_element_type=f32)
    return lax.dot_general(a, b, dims, preferred_element_type=f32)


def norm_rows(h):
    wide = h.astype(f32)
    return (wide * lax.rsqrt(jnp.mean(wide * wide, -ONE, keepdims=True) + 1e-6)).astype(bf)


def run(events):
    for event in events:
        event()


def at_step(i, events):
    for step, functions in events.items():
        pl.when(i == step)(functools.partial(run, functions))


def pair(ref, f):
    return ref.at[pl.ds(TWO * f, TWO)]


def wide(tiles):
    return jnp.concatenate(tiles, axis=ONE)


def down_block(tiles):
    last = [wide([tiles[ROWS + TWO * g + e][FOUR * c : FOUR * c + FOUR] for c in range(FOUR) for e in (ZERO, ONE)]) for g in range(THREE)]
    return jnp.concatenate([wide(tiles[:EIGHT]), wide(tiles[EIGHT:ROWS]), *last], axis=ZERO)


def plan_forward():
    tiles = [max(n for _, n in cols) for cols in (*GU0, DD, DD, *GU1)]
    per_tile = (0.27, 0.36, 0.18, 1.43, 0.72, 0.0, 0.0)
    due = {ZERO: ZERO, ONE: TWO, TWO: SIX, THREE: N_F, FOUR: N_F + TWO, FIVE: 99, SIX: 99}
    length = [3.0] * N_F + [3.8] * (TWO * N_T)
    late = (2.7, 2.7, 2.7, 2.7, 2.7, 1.5, 0.0)
    following = [ZERO] * SEVEN
    arrives = [0.0] * SEVEN
    plan = [[] for _ in range(N_F + TWO * N_T + TWO)]
    now, link = 0.0, 0.0

    def allowed(place, k):
        e = following[k]
        if e > SIX:
            return False
        if k == ZERO:
            return True
        before = following[k - ONE]
        if place == ZERO and k > TWO:
            return False
        return before > FOUR or (before > THREE and link <= now + 1.0) if e == THREE else before > ZERO

    def run_one(place, k):
        nonlocal now, link
        e = following[k]
        now = max(now, arrives[k]) + 0.3
        plan[place].append((k, e))
        link = max(link, now) + per_tile[e] * tiles[k]
        arrives[k] = (link if e < FIVE else now) + late[e]
        following[k] = e + ONE

    for place in range(len(plan)):
        while True:
            ready = [k for k in range(SEVEN) if allowed(place, k) and arrives[k] <= now]
            if ready:
                run_one(place, ready[ZERO])
                continue
            must = [k for k in range(SEVEN) if following[k] < SEVEN and (due[k] <= place or place == len(plan) - ONE)]
            if not must:
                break
            waiting = [k for k in range(SEVEN) if allowed(place, k) and following[k] < SEVEN]
            run_one(place, min(waiting, key=lambda k: arrives[k]))
        if place < len(length):
            now += length[place]
    return plan


def forward_kernel(
    x_hbm, dy_hbm, w_gate, w_up, own_d,
    gu0, d0, gu1, gate0, up0, act0, a0, h1, a1, dact1, d1,
    x, a, big, wt, go, raw, wc, ho, dyt, own,
    ssem, rsem, csem, xsem, wsem, gsem, bsem, rawsem, hsem, asem, dsem, esem,
):
    load_x = pltpu.make_async_copy(x_hbm, x, xsem.at[ZERO])
    load_x.start()

    def own_tile(c, _):
        for layer in range(LAYERS):
            for k, w in enumerate((w_gate, w_up)):
                own[layer, k, c] = w[layer, :, pl.ds(pl.multiple_of(c * L, L), L)]
        return ZERO

    lax.fori_loop(ZERO, C, own_tile, ZERO)
    me = coords()
    barrier(me)

    def stream(k, shard, out, cols):
        g = Gather(me, shard, out, ssem.at[k], rsem.at[k], csem.at[k], cols)
        return g, g.events()

    todo = [(own.at[ZERO], gu0, cols) for cols in GU0] + [(own_d.at[n], d, DD) for n, d in enumerate((d0, d1))] + [(own.at[ONE], gu1, cols) for cols in GU1]
    streams = [stream(k, *one) for k, one in enumerate(todo)]
    plan = [[streams[k][ONE][e] for k, e in place] for place in plan_forward()]

    run(plan[ZERO][:TWO])
    load_x.wait()

    def norm0(t, _):
        rows = pl.ds(pl.multiple_of(t * M, M), M)
        a[rows, :] = norm_rows(x[rows, :])
        return ZERO

    lax.fori_loop(ZERO, N_T, norm0, ZERO)
    keep_a0 = pltpu.make_async_copy(a, a0, xsem.at[ONE])
    keep_a0.start()
    run(plan[ZERO][TWO:])

    def load_w(w, f, slot):
        return pltpu.make_async_copy(w.at[:, pl.ds(TWO * f, TWO)], wt.at[slot], wsem.at[slot])

    def put(f, slot):
        return (
            pltpu.make_async_copy(go.at[slot, ZERO], pair(gate0, f), gsem.at[slot, ZERO]),
            pltpu.make_async_copy(go.at[slot, ONE], pair(up0, f), gsem.at[slot, ONE]),
            pltpu.make_async_copy(pair(big, f), pair(act0, f), bsem.at[slot]),
        )

    def gate_up(f, events, w, finish):
        slot = lax.rem(f, TWO)
        load_w(w, f, slot).wait()

        @pl.when(f + ONE < N_F)
        def _():
            load_w(w, f + ONE, ONE - slot).start()

        finish(f, slot, [wide([wt[slot, k, e].reshape(D, L) for e in (ZERO, ONE)]) for k in (ZERO, ONE)])
        at_step(f, events)
        return ZERO

    def finish0(f, slot, w):
        @pl.when(f >= TWO)
        def _():
            for copy in put(f - TWO, slot):
                copy.wait()

        for t in range(N_T):
            rows = pl.ds(t * M, M)
            gate, up = dot(a[rows, :], w[ZERO]), dot(a[rows, :], w[ONE])
            act = (gate * jax.nn.sigmoid(gate) * up).astype(bf)
            for e in (ZERO, ONE):
                lanes = slice(L * e, L * e + L)
                go[slot, ZERO, e, rows, :] = gate[:, lanes]
                go[slot, ONE, e, rows, :] = up[:, lanes]
                big[TWO * f + e, rows, :] = act[:, lanes]
        for copy in put(f, slot):
            copy.start()

    load_raw = [pltpu.make_async_copy(d, raw, rawsem) for d in (d0, d1)]
    ev = {f: plan[ONE + f] for f in range(N_F)}
    load_w(gu0, ZERO, ZERO).start()
    lax.fori_loop(ZERO, N_F, lambda f, _: gate_up(f, ev, gu0, finish0), ZERO)
    load_raw[ZERO].start()
    for f in (N_F - TWO, N_F - ONE):
        for copy in put(f, f % TWO):
            copy.wait()
    keep_a0.wait()

    def convert():
        def four(g, _):
            blocks = [down_block([raw[c // ELEVEN, c % ELEVEN, g // FOUR, lax.rem(g, FOUR), z] for c in range(C)]) for z in range(FOUR)]
            wc[pl.ds(pl.multiple_of(176 * g, 176), 176), :] = jnp.concatenate(blocks, axis=ZERO)
            return ZERO

        lax.fori_loop(ZERO, ROWS, four, ZERO)

    load_raw[ZERO].wait()
    convert()

    def put_h(t, slot):
        return pltpu.make_async_copy(ho.at[slot], h1.at[pl.ds(pl.multiple_of(t * M, M), M)], hsem.at[slot])

    def load_dy(t, slot):
        return pltpu.make_async_copy(dy_hbm.at[pl.ds(pl.multiple_of(t * M, M), M)], dyt.at[slot], dsem.at[slot])

    def down(t, events):
        slot = lax.rem(t, TWO)

        @pl.when(t >= TWO)
        def _():
            put_h(t - TWO, slot).wait()

        rows = pl.ds(pl.multiple_of(t * M, M), M)
        h = (x[rows, :].astype(f32) + dot(wide([big[c, rows, :] for c in range(C)]), wc[...]).astype(bf).astype(f32)).astype(bf)
        ho[slot] = h
        a[rows, :] = norm_rows(h)
        put_h(t, slot).start()
        at_step(t, events)
        return ZERO

    lax.fori_loop(ZERO, N_T, lambda t, _: down(t, {ZERO: plan[ONE + N_F], ONE: [*plan[TWO + N_F], load_raw[ONE].start], TWO: plan[THREE + N_F], THREE: plan[FOUR + N_F]}), ZERO)
    keep_a1 = pltpu.make_async_copy(a, a1, asem)
    keep_a1.start()
    load_dy(ZERO, ZERO).start()
    for t in (N_T - TWO, N_T - ONE):
        put_h(t, t % TWO).wait()
    load_raw[ONE].wait()
    convert()

    def put_dact(t):
        r = pl.ds(pl.multiple_of(t * M, M), M)
        return pltpu.make_async_copy(big.at[:, r], dact1.at[:, r], esem.at[t])

    def dact(t, events):
        slot = lax.rem(t, TWO)
        load_dy(t, slot).wait()

        @pl.when(t + ONE < N_T)
        def _():
            load_dy(t + ONE, ONE - slot).start()

        rows = pl.ds(pl.multiple_of(t * M, M), M)
        for half in (ZERO, ONE):
            v = dot(dyt[slot], wc[FF // TWO * half : FF // TWO * half + FF // TWO, :], NT).astype(bf)
            for c in range(ELEVEN):
                big[ELEVEN * half + c, rows, :] = v[:, L * c : L * c + L]
        put_dact(t).start()
        at_step(t, events)
        return ZERO

    lax.fori_loop(ZERO, N_T, lambda t, _: dact(t, {n: plan[FIVE + N_F + n] for n in range(N_T)}), ZERO)
    run(plan[-ONE])

    for t in range(N_T):
        put_dact(t).wait()
    keep_a1.wait()
    for g, _ in streams:
        g.finish()


def forward(x, dy, w_gate, w_up, own_d):
    sd = jax.ShapeDtypeStruct
    tall, tall32, narrow = sd((C, T, L), bf), sd((C, T, L), f32), sd((T, D), bf)
    blocks = sd((TWO, C, FOUR, FOUR, FOUR, ROWS, L), bf)
    half_blocks = sd((TWO, C // TWO, FOUR, FOUR, FOUR, ROWS, L), bf)
    dma = pltpu.SemaphoreType.DMA
    return pl.pallas_call(
        forward_kernel,
        in_specs=[HBM, HBM, VMEM, VMEM, VMEM],
        out_specs=[HBM] * ELEVEN,
        out_shape=[blocks, half_blocks, blocks, tall32, tall32, tall, narrow, narrow, narrow, tall, half_blocks],
        scratch_shapes=[
            pltpu.VMEM((T, D), bf), pltpu.VMEM((T, D), bf), pltpu.VMEM((C, T, L), bf),
            pltpu.VMEM((TWO, TWO, TWO, FOUR, FOUR, FOUR, ROWS, L), bf), pltpu.VMEM((TWO, TWO, TWO, T, L), f32),
            pltpu.VMEM((TWO, C // TWO, FOUR, FOUR, FOUR, ROWS, L), bf), pltpu.VMEM((FF, D), bf), pltpu.VMEM((TWO, M, D), bf),
            pltpu.VMEM((TWO, M, D), bf), pltpu.VMEM((LAYERS, TWO, C, ROWS, L), bf),
            dma((SEVEN, THREE, 15)), dma((SEVEN, THREE, 15)), dma((SEVEN, THREE)), dma((TWO,)), dma((TWO,)), dma((TWO, TWO)), dma((TWO,)), dma(()), dma((TWO,)), dma(()), dma((TWO,)), dma((FOUR,)),
        ],
        compiler_params=pltpu.CompilerParams(collective_id=ZERO, has_side_effects=True, vmem_limit_bytes=63 * TWO**20),
        name="forward",
    )(x, dy, w_gate, w_up, own_d)[:TEN]


HALF = FF // TWO
PARTS = ((ZERO, FOUR), (FOUR, FOUR), (EIGHT, THREE))
UNITS = TWELVE


class Scatter:
    @staticmethod
    def vw(p, v, w):
        return (slice(None), v, w) if PERM[p][ONE] < PERM[p][TWO] else (slice(None), w, v)

    @staticmethod
    def scratch():
        s = []
        for p, (_, n) in enumerate(PARTS):
            _, *h = Scatter.vw(p, TWO, FOUR)
            s += [
                pltpu.VMEM((TWO, SIX, n, *h, ROWS, L), bf),
                pltpu.VMEM((TWO, FOUR, n, *h, ROWS, L), bf),
                pltpu.VMEM((n, FOUR, FOUR, ROWS, L), f32), pltpu.VMEM((n, FOUR, FOUR, ROWS, L), bf),
                pltpu.VMEM((SIX, n, TWO, ROWS, L), bf), pltpu.VMEM((TWO, n, TWO, ROWS, L), bf),
                pltpu.VMEM((n, FOUR, ROWS, L), f32), pltpu.VMEM((n, FOUR, ROWS, L), bf),
                pltpu.VMEM((THREE, n, ROWS, L), bf),
            ]
        dma = pltpu.SemaphoreType.DMA
        regular = pltpu.SemaphoreType.REGULAR
        return s + [pltpu.VMEM((ROWS, FF // TWO), bf), dma((TWO, THREE, 15)), dma((TWO, THREE, 15)), dma((TWO, THREE, FOUR)), dma(()), regular((THREE, TWO)), regular((THREE, TWO)), regular((THREE, THREE))]

    def __init__(self, me, grads, out, bufs):
        self.me, self.grads, self.out = me, grads, out
        self.b = [bufs[NINE * p : NINE * p + NINE] for p in range(THREE)]
        self.res, self.ssem, self.rsem, self.lsem, self.osem, self.credit1, self.credit2, self.credit3 = bufs[27:]

    def m(self, p, k, d=ZERO):
        return self.me.plus[PERM[p][k]][d]

    def at_unit(self, k):
        self.k, self.slot = k, lax.rem(k, TWO)
        odd = lax.rem(k, TWO)
        self.grad = jnp.where(k < FOUR, ONE + odd, jnp.where(k < SIX, ZERO, jnp.where(k < EIGHT, THREE, FOUR + odd)))
        self.col0 = C // TWO * jnp.where(k < FOUR, k // TWO, jnp.where(k < EIGHT, odd, k // TWO - FOUR))

    def cols(self, p):
        c, n = PARTS[p]
        return pl.ds(self.col0 + c, n)

    def term(self, p, u, half):
        i = [None] * THREE
        a, v, w = PERM[p]
        i[a], i[v], i[w] = u, pl.ds(TWO * half, TWO), slice(None)
        return self.grads.at[(self.grad, self.cols(p), *i)]

    def own(self, p, j):
        u, h = ((ONE, ZERO), (THREE, ONE), (ZERO, ZERO), (ZERO, ONE))[j]
        return pltpu.make_async_copy(self.term(p, self.m(p, ZERO, u), h), self.b[p][ONE].at[self.slot, j], self.lsem.at[self.slot, p, j])

    def cp(self, p, k):
        b, s = self.b[p], self.slot
        if k < SIX:
            ax, d = ZERO, (ONE, THREE, ONE, THREE, ONE, THREE)[k]
            if k < FOUR:
                u, h = ((TWO, ZERO), (TWO, ONE), (ONE, ONE), (THREE, ZERO))[k]
                src = self.term(p, self.m(p, ZERO, u), h)
            else:
                src = b[ONE].at[s, k - FOUR]
            dst = b[ZERO].at[s, k]
        elif k < TWELVE:
            j = k - SIX
            ax, d = ONE, (ONE, THREE, ONE, THREE, ONE, THREE)[j]
            if j < FOUR:
                v, h = ((TWO, ZERO), (TWO, ONE), (ONE, ONE), (THREE, ZERO))[j]
                src = b[THREE].at[self.vw(p, self.m(p, ONE, v), pl.ds(TWO * h, TWO))]
            else:
                src = b[FIVE].at[j - FOUR]
            dst, s = b[FOUR].at[j], ZERO
        else:
            ax, d = TWO, (ONE, THREE, TWO)[k - TWELVE]
            src, dst, s = b[SEVEN].at[:, self.m(p, TWO, d)], b[EIGHT].at[k - TWELVE], ZERO
        return pltpu.make_async_remote_copy(
            src_ref=src, dst_ref=dst, send_sem=self.ssem.at[s, p, k], recv_sem=self.rsem.at[s, p, k],
            device_id=shifted(self.me, PERM[p][ax], d), device_id_type=MESH,
        )

    def give(self, credit, axis, last):
        @pl.when(self.k < last)
        def _():
            for p in range(THREE):
                for j, d in enumerate((THREE, ONE, TWO)[: credit.shape[ONE]]):
                    pl.semaphore_signal(credit.at[p, j], inc=ONE, device_id=shifted(self.me, PERM[p][axis], d), device_id_type=MESH)

    def take(self, credit, first):
        @pl.when(self.k >= first)
        def _():
            for p in range(THREE):
                for j in range(credit.shape[ONE]):
                    pl.semaphore_wait(credit.at[p, j], ONE)

    def begin(self):
        self.take(self.credit1, TWO)
        for k in (ZERO, ONE, TWO, THREE):
            for p in range(THREE):
                self.cp(p, k).start()
        for p in range(THREE):
            for j in range(FOUR):
                self.own(p, j).start()

    def pass_on(self):
        s = self.slot
        for p in range(THREE):
            b = self.b[p]
            for k in (ZERO, ONE):
                self.own(p, k).wait()
                self.cp(p, k).wait_recv()
                b[ONE][s, k] = (b[ZERO][s, k].astype(f32) + b[ONE][s, k].astype(f32)).astype(bf)
        for k in (FOUR, FIVE):
            for p in range(THREE):
                self.cp(p, k).start()

    def first_sum(self):
        s = self.slot
        for p in range(THREE):
            b = self.b[p]
            for k in (TWO, THREE, FOUR, FIVE):
                self.cp(p, k).wait_recv()
            for j in (TWO, THREE):
                self.own(p, j).wait()
            for half in (ZERO, ONE):
                own, sums, raw = ((TWO, FOUR, THREE), (THREE, FIVE, TWO))[half]
                t = b[ONE][s, own].astype(f32) + b[ZERO][s, sums].astype(f32) + b[ZERO][s, raw].astype(f32)
                ix = self.vw(p, slice(TWO * half, TWO * half + TWO), slice(None))
                b[TWO][ix] = t
                b[THREE][ix] = t.astype(bf)
        for p in range(THREE):
            for k in range(SIX):
                self.cp(p, k).wait_send()
        self.give(self.credit1, ZERO, UNITS - TWO)
        self.take(self.credit2, ONE)
        for k in (SIX, SEVEN, EIGHT, NINE):
            for p in range(THREE):
                self.cp(p, k).start()

    def pass_on2(self):
        for p in range(THREE):
            b = self.b[p]
            for half in (ZERO, ONE):
                self.cp(p, SIX + half).wait_recv()
                v = self.m(p, ONE, (ONE, THREE)[half])
                own = b[TWO][self.vw(p, v, slice(TWO * half, TWO * half + TWO))]
                b[FIVE][half] = (b[FOUR][half].astype(f32) + own).astype(bf)
        for k in (TEN, ELEVEN):
            for p in range(THREE):
                self.cp(p, k).start()

    def second_sum(self):
        for p in range(THREE):
            b, v = self.b[p], self.m(p, ONE)
            for k in (EIGHT, NINE, TEN, ELEVEN):
                self.cp(p, k).wait_recv()
            for half in (ZERO, ONE):
                sums, raw = ((FOUR, THREE), (FIVE, TWO))[half]
                part = slice(TWO * half, TWO * half + TWO)
                t = b[TWO][self.vw(p, v, part)] + b[FOUR][sums].astype(f32) + b[FOUR][raw].astype(f32)
                b[SIX][:, part] = t
                b[SEVEN][:, part] = t.astype(bf)
        for p in range(THREE):
            for k in range(SIX, TWELVE):
                self.cp(p, k).wait_send()
        self.give(self.credit2, ONE, UNITS - ONE)
        self.take(self.credit3, ONE)
        for k in (TWELVE, 13, 14):
            for p in range(THREE):
                self.cp(p, k).start()

    def total(self):
        for p in range(THREE):
            b, w = self.b[p], self.m(p, TWO)
            for k in (TWELVE, 13, 14):
                self.cp(p, k).wait_recv()
            t = b[SIX][:, w]
            for j in range(THREE):
                t = t + b[EIGHT][j].astype(f32)
            c, n = PARTS[p]
            for q in range(n):
                self.res[:, L * (c + q) : L * (c + q) + L] = t[q].astype(bf)
        layer, kind = ONE - self.grad // THREE, lax.rem(self.grad, THREE)
        for m, out in enumerate(self.out):

            @pl.when(kind == m)
            def _():
                pltpu.make_async_copy(self.res, out.at[layer, :, pl.ds(pl.multiple_of(self.col0 * L, L), FF // TWO)], self.osem).start()

        for p in range(THREE):
            for k in (TWELVE, 13, 14):
                self.cp(p, k).wait_send()
        self.give(self.credit3, TWO, UNITS - ONE)
        pltpu.make_async_copy(self.res, self.out[ZERO].at[ZERO, :, pl.ds(ZERO, FF // TWO)], self.osem).wait()

    def tick(self, j, plan):
        def due(steps):
            words = [sum(ONE << (n - 30 * w) for n in steps if n // 30 == w) for w in range(max(steps) // 30 + ONE)]
            word = functools.reduce(lambda have, w: jnp.where(j >= 30 * w, words[w], have), range(ONE, len(words)), words[ZERO])
            return (lax.shift_right_logical(jnp.int32(word), lax.rem(j, 30)) & ONE) == ONE

        @pl.when(due({n for steps in plan.values() for n in steps}))
        def _():
            for event in (self.total, self.second_sum, self.pass_on2, self.first_sum, self.pass_on, self.begin):
                steps = plan[event.__name__]

                @pl.when(due(steps))
                def _():
                    self.at_unit(sum(jnp.where(j > n, ONE, ZERO) for n in steps))
                    event()


S1, S2, S3, S6, S5, S7, S9, TAIL = ZERO, ELEVEN, 19, 35, 43, 51, 63, 79


def make_plan():
    length = [5.2] * ELEVEN + [2.3] * EIGHT + [1.95] * ROWS + [2.3] * EIGHT + [2.1] * EIGHT + [3.6] * TWELVE + [1.95] * ROWS
    ready = [SEVEN, SEVEN, S2 + ONE, S2 + ONE, S3 + ONE, S3 + ONE, S5 + ONE, S5 + ONE, S7 + EIGHT, S7 + EIGHT, S9 + ONE, S9 + ONE]
    names = ("begin", "pass_on", "first_sum", "pass_on2", "second_sum", "total")
    sends = (5.9, 2.95, 1.5, 0.8, 1.0, 0.0)
    late = 2.5
    plan = {name: [] for name in names}
    arrives = [[0.0] * SEVEN for _ in range(UNITS)]
    now, link, step = 3.0, 0.0, ZERO

    def may_run(e, k):
        n = len(plan[names[e]])
        if n != k or (plan[names[e]] and plan[names[e]][-ONE] == step):
            return False
        if e == ZERO:
            return step >= ready[k] and (k < TWO or len(plan["first_sum"]) > k - TWO)
        if len(plan[names[e - ONE]]) <= k or plan[names[e - ONE]][k] == step:
            return False
        if e == TWO and len(plan["second_sum"]) < k:
            return False
        return not (e == FOUR and len(plan["total"]) < k)

    while len(plan["total"]) < UNITS:
        ran = False
        for e in (FIVE, FOUR, THREE, TWO, ONE, ZERO):
            k = len(plan[names[e]])
            if k < UNITS and may_run(e, k) and (arrives[k][e] <= now or step >= TAIL):
                if step >= TAIL and arrives[k][e] > now:
                    if ran or any(may_run(o, len(plan[names[o]])) and arrives[len(plan[names[o]])][o] < arrives[k][e] for o in range(SIX) if o != e and len(plan[names[o]]) < UNITS):
                        continue
                    now = arrives[k][e]
                plan[names[e]].append(step)
                ran = True
                now += 0.3
                link = max(link, now) + sends[e]
                if e == ZERO:
                    arrives[k][ONE], arrives[k][TWO] = link - sends[ONE] + late, link + late
                elif e < FIVE:
                    arrives[k][e + ONE] = max(arrives[k][e + ONE], link + late)
        now += length[step] if step < TAIL else 0.05
        step += ONE
    return plan


PLAN = make_plan()
N_STEPS = max(PLAN["total"]) + ONE


def backward_kernel(
    x, dy, gu0, d0, gu1, gate0, up0, act0, a0, h1, a1, dact1,
    dx, by_down, by_gate, by_up, grads, dup1,
    am, dh, r1, r2, r3, stg, tl, ob, gl, ht,
    lsem, r1sem, r2sem, r3sem, amsem, wsem, dasem, tlsem, obsem, glsem, flsem, hsem, dxsem, *bufs,
):
    me = coords()
    barrier(me, sib=False)
    scatter = Scatter(me, grads, (by_down, by_gate, by_up), bufs)

    def rows(t, n=M):
        return pl.ds(pl.multiple_of(t * n, n), n)

    def col(f, n=F):
        return pl.ds(pl.multiple_of(f * n, 128), n)

    load_dh = pltpu.make_async_copy(dy, dh, lsem)
    load_dup = pltpu.make_async_copy(dup1, r1, r1sem)
    load_act = pltpu.make_async_copy(act0, r2, r2sem)

    def load_am(src):
        return pltpu.make_async_copy(src, am, amsem)

    def load_wt(f, slot):
        return [
            pltpu.make_async_copy(gu1.at[k, pl.ds(TWO * f, TWO), pl.ds(TWO * h, TWO)], stg.at[pl.ds(EIGHT * slot + FOUR * k + TWO * h, TWO)], wsem.at[slot, k, h])
            for k in (ZERO, ONE) for h in (ZERO, ONE)
        ]

    def load_dact(f, slot):
        return pltpu.make_async_copy(pair(dact1, f), pair(r1, f), dasem.at[slot])

    def load_r3(src, h):
        return pltpu.make_async_copy(src.at[:, pl.ds(TWO * h, TWO)], r3.at[:, pl.ds(TWO * h, TWO)], r3sem.at[h])

    def flush(grad, half):
        return pltpu.make_async_copy(stg, grads.at[grad, :, pl.ds(TWO * half, TWO)], flsem)

    def put_tl(f, slot):
        return pltpu.make_async_copy(tl.at[slot], pair(dup1, f), tlsem.at[slot])

    def put_ob(grad, f, slot):
        return [pltpu.make_async_copy(ob.at[slot, k], grads.at[grad + k, pl.ds(TWO * f, TWO)], obsem.at[slot, k]) for k in (ZERO, ONE)]

    def load_gl(f, e):
        return [pltpu.make_async_copy(src.at[TWO * f + e], gl.at[e, k], glsem.at[e, k]) for k, src in enumerate((gate0, up0))]

    def load_h(src, t):
        return pltpu.make_async_copy(src.at[rows(t)], ht, hsem)

    def put_dx(t):
        return pltpu.make_async_copy(dh.at[rows(t)], dx.at[rows(t)], dxsem.at[t])

    def go(copies):
        for c in copies:
            c.start()

    def done(copies):
        for c in copies:
            c.wait()

    def when(condition, f):
        pl.when(condition)(f)

    def gate_up_grad(slot, tiles, parts=(ZERO, FOUR)):
        lo, hi = parts
        v = dot(am[:, F * lo : F * hi], wide(tiles), TN).astype(bf)
        for k in (ZERO, ONE):
            for e in (ZERO, ONE):
                ob[slot, k, e, lo:hi] = v[:, F * k + L * e : F * k + L * e + L].reshape(hi - lo, FOUR, FOUR, ROWS, L)

    def layer1(f, slot):
        w = []
        for k in (ZERO, ONE):
            halves = [wide([stg[EIGHT * slot + FOUR * k + TWO * h + e].reshape(D // TWO, L) for e in (ZERO, ONE)]) for h in (ZERO, ONE)]
            w.append(jnp.concatenate(halves, axis=ZERO))
        for t in range(N_T):
            r = pl.ds(t * M, M)
            gate, up = dot(am[r, :], w[ZERO]), dot(am[r, :], w[ONE])
            by_act = wide([r1[TWO * f + e, r, :] for e in (ZERO, ONE)]).astype(f32)
            sig = jax.nn.sigmoid(gate)
            silu = gate * sig
            act, by_gate, by_up = silu * up, by_act * up * (sig + silu * (ONE - sig)), by_act * silu
            for e in (ZERO, ONE):
                lanes = slice(L * e, L * e + L)
                r1[TWO * f + e, r, :] = act[:, lanes].astype(bf)
                r2[TWO * f + e, r, :] = by_gate[:, lanes].astype(bf)
                tl[slot, e, r, :] = by_up[:, lanes].astype(bf)
        gate_up_grad(slot, [r2[TWO * f], r2[TWO * f + ONE], tl[slot, ZERO], tl[slot, ONE]])

    def down_grad(s, src, grad):
        half, c = s // FOUR, lax.rem(s, FOUR)
        lhs = wide([src[C // TWO * half + i] for i in range(C // TWO)])
        am[: FF // TWO, :F] = dot(lhs, dh[:, col(c)], TN).astype(bf)
        when(s == FOUR, lambda: flush(grad, ZERO).wait())
        lanes = [slice(L * e, L * e + L) for e in (ZERO, ONE)]

        def four(g, _):
            v = am[pl.ds(pl.multiple_of(176 * g, 176), 176), :F]
            x, y = g // FOUR, lax.rem(g, FOUR)
            for z in range(FOUR):
                for e in (ZERO, ONE):
                    stg[TWO * c + e, x, y, z] = v[44 * z : 44 * z + ROWS, lanes[e]]
                    stg[EIGHT + TWO * c + e, x, y, z] = v[44 * z + ROWS : 44 * z + 32, lanes[e]]
            for k in range(FOUR):

                @pl.when(c == k)
                def _():
                    for z in range(FOUR):
                        for n in range(THREE):
                            for e in (ZERO, ONE):
                                stg[ROWS + TWO * n + e, x, y, z, FOUR * k : FOUR * k + FOUR] = v[44 * z + 32 + FOUR * n : 44 * z + 36 + FOUR * n, lanes[e]]

            return ZERO

        lax.fori_loop(ZERO, EIGHT, four, ZERO)
        for h in (ZERO, ONE):
            when(s == FOUR * h + THREE, lambda: flush(grad, h).start())

    def silu_back(f, e, t):
        r = pl.ds(t * M, M)
        gate, up, by_act = gl[e, ZERO, r, :], gl[e, ONE, r, :], r1[TWO * f + e, r, :].astype(f32)
        sig = jax.nn.sigmoid(gate)
        silu = gate * sig
        r2[TWO * f + e, r, :] = (by_act * up * (sig + silu * (ONE - sig))).astype(bf)
        r1[TWO * f + e, r, :] = (by_act * silu).astype(bf)

    def by_input(src, n, t):
        w = wide([r3[c, pl.ds(TWO * n, TWO)].reshape(D // TWO, L) for c in range(C)])
        return dot(wide([src[c, rows(t), :] for c in range(C)]), w, NT).astype(bf)

    def norm_back(t):
        h = ht[...].astype(f32)
        by_a = am[rows(t), :].astype(f32)
        scale = lax.rsqrt(jnp.mean(h * h, -ONE, keepdims=True) + 1e-6)
        by_wide = scale * by_a - h * (scale * scale * scale * jnp.mean(h * by_a, -ONE, keepdims=True))
        dh[rows(t), :] = (dh[rows(t), :].astype(f32) + by_wide.astype(bf).astype(f32)).astype(bf)

    def down_rows(half):
        def four(g, _):
            blocks = [down_block([r3[c, TWO * half + g // FOUR, lax.rem(g, FOUR), z] for c in range(C)]) for z in range(FOUR)]
            am[pl.ds(pl.multiple_of(176 * g, 176), 176), :] = jnp.concatenate(blocks, axis=ZERO)
            return ZERO

        lax.fori_loop(ZERO, EIGHT, four, ZERO)

    def step(j, _):
        def within(a, b):
            return (j >= a) & (j < b)

        in1, in2, in3 = j < S2, within(S2, S3), within(S3, S6)
        in6, in5, in7, in9 = within(S6, S5), within(S5, S7), within(S7, S9), within(S9, TAIL)

        @pl.when(in1)
        def _():
            f = j - S1
            slot = lax.rem(f, TWO)

            @pl.when(f >= TWO)
            def _():
                done(put_ob(ONE, f - TWO, slot))
                put_tl(f - TWO, slot).wait()

            done(load_wt(f, slot))
            load_dact(f, slot).wait()

            @pl.when(f + ONE < N_F)
            def _():
                go(load_wt(f + ONE, ONE - slot))
                load_dact(f + ONE, ONE - slot).start()

            when(f == TWO, lambda: go([load_r3(gu1.at[ZERO], h) for h in (ZERO, ONE)]))

        @pl.when(in2)
        def _():
            @pl.when(j == S2)
            def _():
                done(put_ob(ONE, N_F - TWO, ONE))
                put_tl(N_F - TWO, ONE).wait()
                load_dh.wait()

            @pl.when(j == S2 + ONE)
            def _():
                done(put_ob(ONE, N_F - ONE, ZERO))
                put_tl(N_F - ONE, ZERO).wait()

        def input_pre(s, w, src):
            when(s == ZERO, lambda: load_r3(w.at[ZERO], ZERO).wait())

            @pl.when(s == FOUR)
            def _():
                load_r3(w.at[ZERO], ONE).wait()
                load_r3(w.at[ONE], ZERO).start()

            @pl.when(s == EIGHT)
            def _():
                load_r3(w.at[ONE], ZERO).wait()
                load_r3(w.at[ONE], ONE).start()

            when(s == ELEVEN, lambda: load_h(src, ZERO).start())
            when(s == TWELVE, lambda: load_r3(w.at[ONE], ONE).wait())

        @pl.when(in3)
        def _():
            s = j - S3
            input_pre(s, gu1, h1)
            when(s == ZERO, load_dup.start)
            when(s == ONE, lambda: flush(ZERO, ONE).wait())

            @pl.when(s == EIGHT)
            def _():
                load_dup.wait()
                load_act.start()

            when(s == TWELVE, lambda: load_r3(d0, ZERO).start())

        @pl.when(in9)
        def _():
            s = j - S9
            input_pre(s, gu0, x)
            when(s == ZERO, lambda: done(put_ob(FOUR, N_F - TWO, ONE)))
            when(s == ONE, lambda: done(put_ob(FOUR, N_F - ONE, ZERO)))

        @pl.when(j == S6)
        def _():
            load_act.wait()
            load_r3(d0, ONE).start()

        @pl.when(in5)
        def _():
            s = j - S5

            @pl.when(s == ZERO)
            def _():
                load_r3(d0, ZERO).wait()
                go(load_gl(ZERO, ZERO) + load_gl(ZERO, ONE))

            @pl.when(s == ONE)
            def _():
                flush(THREE, ONE).wait()
                load_r3(gu0.at[ZERO], ZERO).start()

            when(s == FOUR, lambda: load_r3(d0, ONE).wait())
            when(s == FIVE, lambda: load_r3(gu0.at[ZERO], ONE).start())

        @pl.when(in7)
        def _():
            when(j == S7 + ONE, lambda: load_am(a0).wait())
            when(j >= S7 + THREE, lambda: done(put_ob(FOUR, j - S7 - THREE, lax.rem(j - S7 - THREE, TWO))))

        scatter.tick(j, PLAN)

        @pl.when(in1)
        def _():
            f = j - S1
            slot = lax.rem(f, TWO)
            layer1(f, slot)
            go(put_ob(ONE, f, slot))
            put_tl(f, slot).start()

        when(in2, lambda: down_grad(j - S2, r1, ZERO))
        when(in6, lambda: down_grad(j - S6, r2, THREE))

        @pl.when(in3 | in9)
        def _():
            s = jnp.where(in3, j - S3, j - S9)
            n, t = lax.rem(s, EIGHT) // FOUR, lax.rem(s, FOUR)
            here = (rows(t), col(n, D // TWO))

            def more():
                am[here] = (am[here].astype(f32) + by_input(r1, n, t).astype(f32)).astype(bf)

            @pl.when(s < EIGHT)
            def _():
                am[here] = by_input(r2, n, t)

            when((s >= EIGHT) & (s < 13), more)

            @pl.when(s >= 13)
            def _():
                load_h(h1, t - ONE).wait()
                norm_back(t - ONE)
                more()
                when(in3, lambda: load_h(h1, t).start())
                when(in9, lambda: load_h(x, t).start())
                when(in9, lambda: put_dx(t - ONE).start())

            @pl.when(s == 15)
            def _():
                load_h(h1, THREE).wait()
                norm_back(THREE)
                when(in9, lambda: put_dx(THREE).start())

        @pl.when(in5)
        def _():
            s = j - S5
            half, t = s // FOUR, lax.rem(s, FOUR)
            when(t == ZERO, lambda: down_rows(half))
            v = dot(dh[rows(t), :], am[: FF // TWO, :], NT).astype(bf)
            for c in range(C // TWO):
                r1[C // TWO * half + c, rows(t), :] = v[:, L * c : L * c + L]
            when(s == SEVEN, lambda: load_am(a0).start())

        @pl.when(in7)
        def _():
            i = j - S7
            before = i - ONE
            slot = lax.rem(i + ONE, TWO)
            tiles = lambda: [r2[TWO * before], r2[TWO * before + ONE], r1[TWO * before], r1[TWO * before + ONE]]

            @pl.when(i == ZERO)
            def _():
                for e in (ZERO, ONE):
                    done(load_gl(ZERO, e))
                    for t in range(FOUR):
                        silu_back(ZERO, e, t)
                    go(load_gl(ONE, e))

            @pl.when((i > ZERO) & (i < N_F))
            def _():
                for e in (ZERO, ONE):
                    done(load_gl(i, e))
                    for t in (ZERO, ONE):
                        gate_up_grad(slot, tiles(), (TWO * e + t, TWO * e + t + ONE))
                        silu_back(i, e, TWO * t)
                        silu_back(i, e, TWO * t + ONE)
                    when(i + ONE < N_F, lambda: go(load_gl(i + ONE, e)))

            when(i == N_F, lambda: gate_up_grad(slot, tiles()))
            when(i > ZERO, lambda: go(put_ob(FOUR, before, slot)))

        return ZERO

    load_am(a1).start()
    go(load_wt(ZERO, ZERO))
    load_dact(ZERO, ZERO).start()
    load_dh.start()
    load_am(a1).wait()
    lax.fori_loop(ZERO, N_STEPS, step, ZERO)
    done([put_dx(t) for t in range(FOUR)])


def backward(x, dy, gu0, d0, *args):
    sd = jax.ShapeDtypeStruct
    dma = pltpu.SemaphoreType.DMA
    return pl.pallas_call(
        backward_kernel,
        in_specs=[HBM] * TWELVE,
        out_specs=[HBM] * SIX,
        out_shape=[sd((T, D), bf), *[sd((LAYERS, ROWS, FF), bf)] * THREE, sd((SIX, C, FOUR, FOUR, FOUR, ROWS, L), bf), sd((C, T, L), bf)],
        scratch_shapes=[
            pltpu.VMEM((T, D), bf), pltpu.VMEM((T, D), bf), pltpu.VMEM((C, T, L), bf), pltpu.VMEM((C, T, L), bf),
            pltpu.VMEM((C, FOUR, FOUR, FOUR, ROWS, L), bf), pltpu.VMEM((C, TWO, FOUR, FOUR, ROWS, L), bf), pltpu.VMEM((TWO, TWO, T, L), bf),
            pltpu.VMEM((TWO, TWO, TWO, FOUR, FOUR, FOUR, ROWS, L), bf), pltpu.VMEM((TWO, TWO, T, L), f32), pltpu.VMEM((M, D), bf),
            dma(()), dma(()), dma(()), dma((TWO,)), dma(()), dma((TWO, TWO, TWO)), dma((TWO,)), dma((TWO,)), dma((TWO, TWO)), dma((TWO, TWO)), dma(()), dma(()), dma((FOUR,)),
            *Scatter.scratch(),
        ],
        compiler_params=pltpu.CompilerParams(collective_id=ONE, has_side_effects=True, vmem_limit_bytes=63 * TWO**20 + 900 * 1024),
        name="backward",
    )(x, dy, gu0, d0.reshape(C, FOUR, FOUR, FOUR, ROWS, L), *args)[:FOUR]


def pack_down(t):
    first = t[:, :32].reshape(-ONE, TWO, ROWS, EIGHT, L).transpose(ZERO, ONE, THREE, TWO, FOUR).reshape(-ONE, ROWS, ROWS, L)
    last = t[:, 32:].reshape(-ONE, THREE, FOUR, FOUR, TWO, L).transpose(ZERO, ONE, FOUR, THREE, TWO, FIVE).reshape(-ONE, SIX, ROWS, L)
    return jnp.concatenate([first, last], axis=ONE).reshape(-ONE, TWO, C // TWO, ROWS, L)


def unpack_down(t):
    last = t[:, :, TWO * D :].reshape(-ONE, FOUR, FOUR, THREE, F).transpose(ZERO, THREE, TWO, ONE, FOUR).reshape(-ONE, TWELVE, D)
    return jnp.concatenate([t[:, :, :D], t[:, :, D : TWO * D], last], axis=ONE)


def solution(mesh):
    def device(x, dy, w_gate, w_up, w_down):
        x, dy = x[ZERO], dy[ZERO]
        own_d = pack_down(w_down)
        gu0, d0, gu1, *rest = forward(x, dy, w_gate, w_up, own_d)
        by_x, by_down, by_gate, by_up = backward(x, dy, gu0, d0, gu1, *rest)
        return by_x[None], by_gate, by_up, unpack_down(by_down)

    return jax.shard_map(
        device,
        mesh=mesh,
        in_specs=(P(("rep", "dp")), P(("rep", "dp")), *(P(None, "dp"),) * THREE),
        out_specs=(P(("rep", "dp")), *(P("rep", "dp"),) * THREE),
        check_vma=False,
    )
```

time: 2040 us -> 406 us (0.20)
  waiting for transfers between devices: 1070 us -> 0 us
  blocking collectives: 448 us -> 0 us
  Pallas kernels: 0 us -> 393 us
  matrix products: 355 us -> 0 us
  other arithmetic: 86.6 us -> 0.71 us
  starting transfers between devices: 32.2 us -> 0 us
    unnamed x26 -> x0, waiting for transfers between devices: 761 us -> none
    unnamed x1 -> x0, blocking collectives: 448 us -> none
    pallas_call x0 -> x2, Pallas kernels: none -> 393 us  [the longest x1 281 us: backward(): pl.pallas_call(backward_kernel, in_specs=[HBM] * TWELVE, out_specs=[HBM]...]
    dot_general x17 -> x0, matrix products: 355 us -> none  [the longest x6 130 us: layer(): up = jnp.dot(a, w['w_up'], preferred_element_type=jnp.float32)]
    squeeze x6 -> x0, waiting for transfers between devices: 306 us -> none  [stack(): h = layer(h, {name: w[number] for name, w in weights.items()})]
    unnamed x5 -> x0, other arithmetic: 66.3 us -> none
    unnamed x16 -> x0, starting transfers between devices: 32 us -> none
  transfers between devices with their start and end apart: 22 -> 0, of which waited for: 9 -> 0; matrix products, arithmetic and copies ran while one was open for 45% -> 0% of each run, Pallas kernels for 0% -> 0%
where the time goes in v3:
time: 406 us; the launch traced here: 405 us
  Pallas kernels  393 us (97%)
  local copies, waits for them, and re-layouts  10.7 us (3%)
    pallas_call x1, Pallas kernels, backward(): pl.pallas_call(backward_kernel, in_specs=[HBM] * TWELVE, out_specs=[HBM]...  281 us
    pallas_call x1, Pallas kernels, forward(): pl.pallas_call(forward_kernel, in_specs=[HBM, HBM, VMEM, VMEM, VMEM], out...  112 us

profile of v3, /device:TPU:0, one launch (start us, length us, event | category | flops | bytes accessed | tf_op | source)
XLA Modules:
  0.0 405.0 jit_solution(867682607903220512)
XLA Ops:
  0.6 0.8 slice.16
  1.5 1.0 slice.15
  2.5 0.1 reshape.32
  2.7 0.7 pad_maximum_fusion.1
  3.4 112.3 %forward.1 = (bf16[2,22,4,4,4,16,128]{6,5,4,3,2,1,0:T(8,128)(2,1)}, bf16[2,11,4,4,4,16,128]{6,5,4,3,2,1,0:T(8,128)(2,1)}, bf16[2,22,4,4,4,16,128]{6,5,4,3,2,1,0:...) custom-call(bf16[2048,1024]{1,0:T(8,128)(2,1)} %bitcast.14, ...), custom_call_target="tpu_custom_call" | custom-call | tf_op jit(solution)/shard_map/forward/pallas_call | solution.py:378
  115.7 280.6 %backward.1 = (bf16[2048,1024]{1,0:T(8,128)(2,1)}, bf16[2,16,2816]{2,1,0:T(8,128)(2,1)}, bf16[2,16,2816]{2,1,0:T(8,128)(2,1)}, bf16[2,16,2816]{2,1,0:T(8,128)(2,...) custom-call(bf16[2048,1024]{1,0:T(8,128)(2,1)} %bitcast.15, ...), custom_call_target="tpu_custom_call" | custom-call | tf_op jit(solution)/shard_map/backward/pallas_call | solution.py:1004
  396.3 0.0 copy-start.1
  396.3 0.0 copy-start
  396.3 0.9 slice.19
  397.1 0.9 fusion
  398.1 0.9 copy.17
  399.0 4.6 %copy.23 = bf16[1,2048,1024]{2,1,0:T(8,128)(2,1)} copy(bf16[1,2048,1024]{2,1,0:T(8,128)(2,1)} %bitcast.19) | data formatting | bytes 8388608
  403.6 0.0 copy-done.1
  403.6 0.7 copy.24
  404.3 0.0 copy-done
  404.3 0.7 copy.25
  (7 shorter events, 0.2 us)
Async XLA Ops:
  396.3 7.4 %copy-start.1 = (bf16[2,16,2816]{2,1,0:T(8,128)(2,1)S(1)}, bf16[2,16,2816]{2,1,0:T(8,128)(2,1)}, u32[]{:S(2)}) copy-start(bf16[2,16,2816]{2,1,0:T(8,128)(2,1)} %get-tuple-element.47) | copy-start | bytes 540676
  396.3 8.1 %copy-start = (bf16[2,16,2816]{2,1,0:T(8,128)(2,1)S(1)}, bf16[2,16,2816]{2,1,0:T(8,128)(2,1)}, u32[]{:S(2)}) copy-start(bf16[2,16,2816]{2,1,0:T(8,128)(2,1)} %get-tuple-element.48) | copy-start | bytes 540676

commit v4 on v3

--- a/solution.py
+++ b/solution.py
@@ -329,7 +329,7 @@
         at_step(t, events)
         return ZERO
 
-    lax.fori_loop(ZERO, N_T, lambda t, _: down(t, {ZERO: plan[ONE + N_F], ONE: [*plan[TWO + N_F], load_raw[ONE].start], TWO: plan[THREE + N_F], THREE: plan[FOUR + N_F]}), ZERO)
+    lax.fori_loop(ZERO, N_T, lambda t, _: down(t, {ZERO: plan[ONE + N_F], ONE: [*plan[TWO + N_F], lambda: load_raw[ONE].start()], TWO: plan[THREE + N_F], THREE: plan[FOUR + N_F]}), ZERO)
     keep_a1 = pltpu.make_async_copy(a, a1, asem)
     keep_a1.start()
     load_dy(ZERO, ZERO).start()
@@ -430,8 +430,8 @@
     def at_unit(self, k):
         self.k, self.slot = k, lax.rem(k, TWO)
         odd = lax.rem(k, TWO)
-        self.grad = jnp.where(k < FOUR, ONE + odd, jnp.where(k < SIX, ZERO, jnp.where(k < EIGHT, THREE, FOUR + odd)))
-        self.col0 = C // TWO * jnp.where(k < FOUR, k // TWO, jnp.where(k < EIGHT, odd, k // TWO - FOUR))
+        self.grad = jnp.where(k < FOUR, ONE + odd, jnp.where(k < SIX, ZERO, jnp.where(k < EIGHT, THREE, k // TWO)))
+        self.col0 = C // TWO * jnp.where(k < FOUR, k // TWO, odd)
 
     def cols(self, p):
         c, n = PARTS[p]
@@ -504,7 +504,8 @@
             for k in (ZERO, ONE):
                 self.own(p, k).wait()
                 self.cp(p, k).wait_recv()
-                b[ONE][s, k] = (b[ZERO][s, k].astype(f32) + b[ONE][s, k].astype(f32)).astype(bf)
+                for n in range(PARTS[p][ONE]):
+                    b[ONE][s, k, n] = (b[ZERO][s, k, n].astype(f32) + b[ONE][s, k, n].astype(f32)).astype(bf)
         for k in (FOUR, FIVE):
             for p in range(THREE):
                 self.cp(p, k).start()
@@ -519,10 +520,11 @@
                 self.own(p, j).wait()
             for half in (ZERO, ONE):
                 own, sums, raw = ((TWO, FOUR, THREE), (THREE, FIVE, TWO))[half]
-                t = b[ONE][s, own].astype(f32) + b[ZERO][s, sums].astype(f32) + b[ZERO][s, raw].astype(f32)
-                ix = self.vw(p, slice(TWO * half, TWO * half + TWO), slice(None))
-                b[TWO][ix] = t
-                b[THREE][ix] = t.astype(bf)
+                _, *ix = self.vw(p, slice(TWO * half, TWO * half + TWO), slice(None))
+                for n in range(PARTS[p][ONE]):
+                    t = b[ONE][s, own, n].astype(f32) + b[ZERO][s, sums, n].astype(f32) + b[ZERO][s, raw, n].astype(f32)
+                    b[TWO][(n, *ix)] = t
+                    b[THREE][(n, *ix)] = t.astype(bf)
         for p in range(THREE):
             for k in range(SIX):
                 self.cp(p, k).wait_send()
@@ -590,7 +592,7 @@
 
     def tick(self, j, plan):
         def due(steps):
-            words = [sum(ONE << (n - 30 * w) for n in steps if n // 30 == w) for w in range(max(steps) // 30 + ONE)]
+            words = [sum(ONE << (n - 30 * w) for n in steps if n // 30 == w) for w in range(max(plan["total"]) // 30 + ONE)]
             word = functools.reduce(lambda have, w: jnp.where(j >= 30 * w, words[w], have), range(ONE, len(words)), words[ZERO])
             return (lax.shift_right_logical(jnp.int32(word), lax.rem(j, 30)) & ONE) == ONE
 
@@ -605,14 +607,14 @@
                     event()
 
 
-S1, S2, S3, S6, S5, S7, S9, TAIL = ZERO, ELEVEN, 19, 35, 43, 51, 63, 79
+S1, S2, S3, S6, S5, S7, S8, S9, TAIL = ZERO, ELEVEN, 19, 35, 43, 51, 63, 74, 90
 
 
 def make_plan():
-    length = [5.2] * ELEVEN + [2.3] * EIGHT + [1.95] * ROWS + [2.3] * EIGHT + [2.1] * EIGHT + [3.6] * TWELVE + [1.95] * ROWS
-    ready = [SEVEN, SEVEN, S2 + ONE, S2 + ONE, S3 + ONE, S3 + ONE, S5 + ONE, S5 + ONE, S7 + EIGHT, S7 + EIGHT, S9 + ONE, S9 + ONE]
+    length = [5.1] * ELEVEN + [2.2] * EIGHT + [1.95] * ROWS + [2.2] * EIGHT + [2.1] * EIGHT + [2.4] * TWELVE + [1.4] * ELEVEN + [1.95] * ROWS
+    ready = [SEVEN, SEVEN, S2 + ONE, S2 + ONE, S3 + ONE, S3 + ONE, S5 + ONE, S5 + ONE, S7 + SEVEN, S8 + ONE, S8 + SEVEN, S9 + ONE]
     names = ("begin", "pass_on", "first_sum", "pass_on2", "second_sum", "total")
-    sends = (5.9, 2.95, 1.5, 0.8, 1.0, 0.0)
+    sends = (6.1, 3.05, 1.6, 0.8, 1.1, 0.0)
     late = 2.5
     plan = {name: [] for name in names}
     arrives = [[0.0] * SEVEN for _ in range(UNITS)]
@@ -641,7 +643,7 @@
                     now = arrives[k][e]
                 plan[names[e]].append(step)
                 ran = True
-                now += 0.3
+                now += 0.35
                 link = max(link, now) + sends[e]
                 if e == ZERO:
                     arrives[k][ONE], arrives[k][TWO] = link - sends[ONE] + late, link + late
@@ -697,8 +699,8 @@
     def put_tl(f, slot):
         return pltpu.make_async_copy(tl.at[slot], pair(dup1, f), tlsem.at[slot])
 
-    def put_ob(grad, f, slot):
-        return [pltpu.make_async_copy(ob.at[slot, k], grads.at[grad + k, pl.ds(TWO * f, TWO)], obsem.at[slot, k]) for k in (ZERO, ONE)]
+    def put_ob(grad, f, slot, kinds=(ZERO, ONE)):
+        return [pltpu.make_async_copy(ob.at[slot, k], grads.at[grad + k, pl.ds(TWO * f, TWO)], obsem.at[slot, k]) for k in kinds]
 
     def load_gl(f, e):
         return [pltpu.make_async_copy(src.at[TWO * f + e], gl.at[e, k], glsem.at[e, k]) for k, src in enumerate((gate0, up0))]
@@ -720,12 +722,12 @@
     def when(condition, f):
         pl.when(condition)(f)
 
-    def gate_up_grad(slot, tiles, parts=(ZERO, FOUR)):
+    def gate_up_grad(slot, tiles, parts=(ZERO, FOUR), kinds=(ZERO, ONE)):
         lo, hi = parts
         v = dot(am[:, F * lo : F * hi], wide(tiles), TN).astype(bf)
-        for k in (ZERO, ONE):
+        for n, k in enumerate(kinds):
             for e in (ZERO, ONE):
-                ob[slot, k, e, lo:hi] = v[:, F * k + L * e : F * k + L * e + L].reshape(hi - lo, FOUR, FOUR, ROWS, L)
+                ob[slot, k, e, lo:hi] = v[:, F * n + L * e : F * n + L * e + L].reshape(hi - lo, FOUR, FOUR, ROWS, L)
 
     def layer1(f, slot):
         w = []
@@ -776,12 +778,13 @@
             when(s == FOUR * h + THREE, lambda: flush(grad, h).start())
 
     def silu_back(f, e, t):
-        r = pl.ds(t * M, M)
-        gate, up, by_act = gl[e, ZERO, r, :], gl[e, ONE, r, :], r1[TWO * f + e, r, :].astype(f32)
-        sig = jax.nn.sigmoid(gate)
-        silu = gate * sig
-        r2[TWO * f + e, r, :] = (by_act * up * (sig + silu * (ONE - sig))).astype(bf)
-        r1[TWO * f + e, r, :] = (by_act * silu).astype(bf)
+        for q in range(t * M, t * M + M, L):
+            r = slice(q, q + L)
+            gate, up, by_act = gl[e, ZERO, r, :], gl[e, ONE, r, :], r1[TWO * f + e, r, :].astype(f32)
+            sig = jax.nn.sigmoid(gate)
+            silu = gate * sig
+            r2[TWO * f + e, r, :] = (by_act * up * (sig + silu * (ONE - sig))).astype(bf)
+            r1[TWO * f + e, r, :] = (by_act * silu).astype(bf)
 
     def by_input(src, n, t):
         w = wide([r3[c, pl.ds(TWO * n, TWO)].reshape(D // TWO, L) for c in range(C)])
@@ -807,7 +810,7 @@
             return (j >= a) & (j < b)
 
         in1, in2, in3 = j < S2, within(S2, S3), within(S3, S6)
-        in6, in5, in7, in9 = within(S6, S5), within(S5, S7), within(S7, S9), within(S9, TAIL)
+        in6, in5, in7, in8, in9 = within(S6, S5), within(S5, S7), within(S7, S8), within(S8, S9), within(S9, TAIL)
 
         @pl.when(in1)
         def _():
@@ -862,7 +865,7 @@
         def _():
             s = j - S3
             input_pre(s, gu1, h1)
-            when(s == ZERO, load_dup.start)
+            when(s == ZERO, lambda: load_dup.start())
             when(s == ONE, lambda: flush(ZERO, ONE).wait())
 
             @pl.when(s == EIGHT)
@@ -876,8 +879,8 @@
         def _():
             s = j - S9
             input_pre(s, gu0, x)
-            when(s == ZERO, lambda: done(put_ob(FOUR, N_F - TWO, ONE)))
-            when(s == ONE, lambda: done(put_ob(FOUR, N_F - ONE, ZERO)))
+            when(s == ZERO, lambda: done(put_ob(FOUR, N_F - TWO, ONE, (ONE,))))
+            when(s == ONE, lambda: done(put_ob(FOUR, N_F - ONE, ZERO, (ONE,))))
 
         @pl.when(j == S6)
         def _():
@@ -904,7 +907,16 @@
         @pl.when(in7)
         def _():
             when(j == S7 + ONE, lambda: load_am(a0).wait())
-            when(j >= S7 + THREE, lambda: done(put_ob(FOUR, j - S7 - THREE, lax.rem(j - S7 - THREE, TWO))))
+            i = j - S7
+            when((i >= THREE) & (i != EIGHT), lambda: done(put_ob(FOUR, i - THREE, lax.rem(i - THREE, TWO), (ZERO,))))
+            when(i == SEVEN, lambda: done(put_ob(FOUR, FIVE, ONE, (ZERO,))))
+
+        @pl.when(in8)
+        def _():
+            f = j - S8
+            when(f == ZERO, lambda: done(put_ob(FOUR, N_F - TWO, ONE, (ZERO,))))
+            when(f == ONE, lambda: done(put_ob(FOUR, N_F - ONE, ZERO, (ZERO,))))
+            when(f >= TWO, lambda: done(put_ob(FOUR, f - TWO, lax.rem(f, TWO), (ONE,))))
 
         scatter.tick(j, PLAN)
 
@@ -964,7 +976,7 @@
             i = j - S7
             before = i - ONE
             slot = lax.rem(i + ONE, TWO)
-            tiles = lambda: [r2[TWO * before], r2[TWO * before + ONE], r1[TWO * before], r1[TWO * before + ONE]]
+            tiles = lambda: [r2[TWO * before], r2[TWO * before + ONE]]
 
             @pl.when(i == ZERO)
             def _():
@@ -979,13 +991,20 @@
                 for e in (ZERO, ONE):
                     done(load_gl(i, e))
                     for t in (ZERO, ONE):
-                        gate_up_grad(slot, tiles(), (TWO * e + t, TWO * e + t + ONE))
+                        gate_up_grad(slot, tiles(), (TWO * e + t, TWO * e + t + ONE), (ZERO,))
                         silu_back(i, e, TWO * t)
                         silu_back(i, e, TWO * t + ONE)
                     when(i + ONE < N_F, lambda: go(load_gl(i + ONE, e)))
 
-            when(i == N_F, lambda: gate_up_grad(slot, tiles()))
-            when(i > ZERO, lambda: go(put_ob(FOUR, before, slot)))
+            when(i == N_F, lambda: gate_up_grad(slot, tiles(), (ZERO, FOUR), (ZERO,)))
+            when(i > ZERO, lambda: go(put_ob(FOUR, before, slot, (ZERO,))))
+
+        @pl.when(in8)
+        def _():
+            f = j - S8
+            slot = lax.rem(f, TWO)
+            gate_up_grad(slot, [r1[TWO * f], r1[TWO * f + ONE]], (ZERO, FOUR), (ONE,))
+            go(put_ob(FOUR, f, slot, (ONE,)))
 
         return ZERO
 

time: 406 us -> 401 us (0.988)
  Pallas kernels: 393 us -> 388 us
    pallas_call x1, Pallas kernels: 281 us -> 276 us  [backward(): pl.pallas_call(backward_kernel, in_specs=[HBM] * TWELVE, out_specs=[HBM]...]
where the time goes in v4:
time: 401 us; the launch traced here: 400 us
  Pallas kernels  388 us (97%)
  local copies, waits for them, and re-layouts  10.7 us (3%)
    pallas_call x1, Pallas kernels, backward(): pl.pallas_call(backward_kernel, in_specs=[HBM] * TWELVE, out_specs=[HBM]...  276 us
    pallas_call x1, Pallas kernels, forward(): pl.pallas_call(forward_kernel, in_specs=[HBM, HBM, VMEM, VMEM, VMEM], out...  112 us

profile of v4, /device:TPU:0, one launch (start us, length us, event | category | flops | bytes accessed | tf_op | source)
XLA Modules:
  0.0 400.2 jit_solution(9995248970610987161)
XLA Ops:
  0.6 0.8 slice.16
  1.5 1.0 slice.15
  2.5 0.1 reshape.32
  2.7 0.7 pad_maximum_fusion.1
  3.4 112.3 %forward.1 = (bf16[2,22,4,4,4,16,128]{6,5,4,3,2,1,0:T(8,128)(2,1)}, bf16[2,11,4,4,4,16,128]{6,5,4,3,2,1,0:T(8,128)(2,1)}, bf16[2,22,4,4,4,16,128]{6,5,4,3,2,1,0:...) custom-call(bf16[2048,1024]{1,0:T(8,128)(2,1)} %bitcast.14, ...), custom_call_target="tpu_custom_call" | custom-call | tf_op jit(solution)/shard_map/forward/pallas_call | solution.py:378
  115.7 275.8 %backward.1 = (bf16[2048,1024]{1,0:T(8,128)(2,1)}, bf16[2,16,2816]{2,1,0:T(8,128)(2,1)}, bf16[2,16,2816]{2,1,0:T(8,128)(2,1)}, bf16[2,16,2816]{2,1,0:T(8,128)(2,...) custom-call(bf16[2048,1024]{1,0:T(8,128)(2,1)} %bitcast.15, ...), custom_call_target="tpu_custom_call" | custom-call | tf_op jit(solution)/shard_map/backward/pallas_call | solution.py:1023
  391.5 0.0 copy-start.1
  391.5 0.0 copy-start
  391.5 0.9 slice.19
  392.4 0.9 fusion
  393.4 0.9 copy.17
  394.3 4.6 %copy.23 = bf16[1,2048,1024]{2,1,0:T(8,128)(2,1)} copy(bf16[1,2048,1024]{2,1,0:T(8,128)(2,1)} %bitcast.19) | data formatting | bytes 8388608
  398.9 0.0 copy-done.1
  398.9 0.7 copy.24
  399.6 0.0 copy-done
  399.6 0.7 copy.25
  (7 shorter events, 0.2 us)
Async XLA Ops:
  391.5 7.4 %copy-start.1 = (bf16[2,16,2816]{2,1,0:T(8,128)(2,1)S(1)}, bf16[2,16,2816]{2,1,0:T(8,128)(2,1)}, u32[]{:S(2)}) copy-start(bf16[2,16,2816]{2,1,0:T(8,128)(2,1)} %get-tuple-element.47) | copy-start | bytes 540676
  391.5 8.1 %copy-start = (bf16[2,16,2816]{2,1,0:T(8,128)(2,1)S(1)}, bf16[2,16,2816]{2,1,0:T(8,128)(2,1)}, u32[]{:S(2)}) copy-start(bf16[2,16,2816]{2,1,0:T(8,128)(2,1)} %get-tuple-element.48) | copy-start | bytes 540676

commit v5 on v4

--- a/solution.py
+++ b/solution.py
@@ -812,39 +812,6 @@
         in1, in2, in3 = j < S2, within(S2, S3), within(S3, S6)
         in6, in5, in7, in8, in9 = within(S6, S5), within(S5, S7), within(S7, S8), within(S8, S9), within(S9, TAIL)
 
-        @pl.when(in1)
-        def _():
-            f = j - S1
-            slot = lax.rem(f, TWO)
-
-            @pl.when(f >= TWO)
-            def _():
-                done(put_ob(ONE, f - TWO, slot))
-                put_tl(f - TWO, slot).wait()
-
-            done(load_wt(f, slot))
-            load_dact(f, slot).wait()
-
-            @pl.when(f + ONE < N_F)
-            def _():
-                go(load_wt(f + ONE, ONE - slot))
-                load_dact(f + ONE, ONE - slot).start()
-
-            when(f == TWO, lambda: go([load_r3(gu1.at[ZERO], h) for h in (ZERO, ONE)]))
-
-        @pl.when(in2)
-        def _():
-            @pl.when(j == S2)
-            def _():
-                done(put_ob(ONE, N_F - TWO, ONE))
-                put_tl(N_F - TWO, ONE).wait()
-                load_dh.wait()
-
-            @pl.when(j == S2 + ONE)
-            def _():
-                done(put_ob(ONE, N_F - ONE, ZERO))
-                put_tl(N_F - ONE, ZERO).wait()
-
         def input_pre(s, w, src):
             when(s == ZERO, lambda: load_r3(w.at[ZERO], ZERO).wait())
 
@@ -861,75 +828,113 @@
             when(s == ELEVEN, lambda: load_h(src, ZERO).start())
             when(s == TWELVE, lambda: load_r3(w.at[ONE], ONE).wait())
 
-        @pl.when(in3)
-        def _():
-            s = j - S3
-            input_pre(s, gu1, h1)
-            when(s == ZERO, lambda: load_dup.start())
-            when(s == ONE, lambda: flush(ZERO, ONE).wait())
-
-            @pl.when(s == EIGHT)
-            def _():
-                load_dup.wait()
-                load_act.start()
-
-            when(s == TWELVE, lambda: load_r3(d0, ZERO).start())
-
-        @pl.when(in9)
-        def _():
-            s = j - S9
-            input_pre(s, gu0, x)
-            when(s == ZERO, lambda: done(put_ob(FOUR, N_F - TWO, ONE, (ONE,))))
-            when(s == ONE, lambda: done(put_ob(FOUR, N_F - ONE, ZERO, (ONE,))))
-
-        @pl.when(j == S6)
-        def _():
-            load_act.wait()
-            load_r3(d0, ONE).start()
-
-        @pl.when(in5)
-        def _():
-            s = j - S5
-
-            @pl.when(s == ZERO)
-            def _():
-                load_r3(d0, ZERO).wait()
-                go(load_gl(ZERO, ZERO) + load_gl(ZERO, ONE))
-
-            @pl.when(s == ONE)
-            def _():
-                flush(THREE, ONE).wait()
-                load_r3(gu0.at[ZERO], ZERO).start()
-
-            when(s == FOUR, lambda: load_r3(d0, ONE).wait())
-            when(s == FIVE, lambda: load_r3(gu0.at[ZERO], ONE).start())
-
-        @pl.when(in7)
-        def _():
-            when(j == S7 + ONE, lambda: load_am(a0).wait())
-            i = j - S7
-            when((i >= THREE) & (i != EIGHT), lambda: done(put_ob(FOUR, i - THREE, lax.rem(i - THREE, TWO), (ZERO,))))
-            when(i == SEVEN, lambda: done(put_ob(FOUR, FIVE, ONE, (ZERO,))))
-
-        @pl.when(in8)
-        def _():
-            f = j - S8
-            when(f == ZERO, lambda: done(put_ob(FOUR, N_F - TWO, ONE, (ZERO,))))
-            when(f == ONE, lambda: done(put_ob(FOUR, N_F - ONE, ZERO, (ZERO,))))
-            when(f >= TWO, lambda: done(put_ob(FOUR, f - TWO, lax.rem(f, TWO), (ONE,))))
+        @pl.when(j < S6)
+        def _():
+            @pl.when(in1)
+            def _():
+                f = j - S1
+                slot = lax.rem(f, TWO)
+
+                @pl.when(f >= TWO)
+                def _():
+                    done(put_ob(ONE, f - TWO, slot))
+                    put_tl(f - TWO, slot).wait()
+
+                done(load_wt(f, slot))
+                load_dact(f, slot).wait()
+
+                @pl.when(f + ONE < N_F)
+                def _():
+                    go(load_wt(f + ONE, ONE - slot))
+                    load_dact(f + ONE, ONE - slot).start()
+
+                when(f == TWO, lambda: go([load_r3(gu1.at[ZERO], h) for h in (ZERO, ONE)]))
+
+            @pl.when(in2)
+            def _():
+                @pl.when(j == S2)
+                def _():
+                    done(put_ob(ONE, N_F - TWO, ONE))
+                    put_tl(N_F - TWO, ONE).wait()
+                    load_dh.wait()
+
+                @pl.when(j == S2 + ONE)
+                def _():
+                    done(put_ob(ONE, N_F - ONE, ZERO))
+                    put_tl(N_F - ONE, ZERO).wait()
+
+            @pl.when(in3)
+            def _():
+                s = j - S3
+                input_pre(s, gu1, h1)
+                when(s == ZERO, lambda: load_dup.start())
+                when(s == ONE, lambda: flush(ZERO, ONE).wait())
+
+                @pl.when(s == EIGHT)
+                def _():
+                    load_dup.wait()
+                    load_act.start()
+
+                when(s == TWELVE, lambda: load_r3(d0, ZERO).start())
+
+        @pl.when((j >= S6) & (j < TAIL))
+        def _():
+            @pl.when(in9)
+            def _():
+                s = j - S9
+                input_pre(s, gu0, x)
+                when(s == ZERO, lambda: done(put_ob(FOUR, N_F - TWO, ONE, (ONE,))))
+                when(s == ONE, lambda: done(put_ob(FOUR, N_F - ONE, ZERO, (ONE,))))
+
+            @pl.when(j == S6)
+            def _():
+                load_act.wait()
+                load_r3(d0, ONE).start()
+
+            @pl.when(in5)
+            def _():
+                s = j - S5
+
+                @pl.when(s == ZERO)
+                def _():
+                    load_r3(d0, ZERO).wait()
+                    go(load_gl(ZERO, ZERO) + load_gl(ZERO, ONE))
+
+                @pl.when(s == ONE)
+                def _():
+                    flush(THREE, ONE).wait()
+                    load_r3(gu0.at[ZERO], ZERO).start()
+
+                when(s == FOUR, lambda: load_r3(d0, ONE).wait())
+                when(s == FIVE, lambda: load_r3(gu0.at[ZERO], ONE).start())
+
+            @pl.when(in7)
+            def _():
+                when(j == S7 + ONE, lambda: load_am(a0).wait())
+                i = j - S7
+                when((i >= THREE) & (i != EIGHT), lambda: done(put_ob(FOUR, i - THREE, lax.rem(i - THREE, TWO), (ZERO,))))
+                when(i == SEVEN, lambda: done(put_ob(FOUR, FIVE, ONE, (ZERO,))))
+
+            @pl.when(in8)
+            def _():
+                f = j - S8
+                when(f == ZERO, lambda: done(put_ob(FOUR, N_F - TWO, ONE, (ZERO,))))
+                when(f == ONE, lambda: done(put_ob(FOUR, N_F - ONE, ZERO, (ZERO,))))
+                when(f >= TWO, lambda: done(put_ob(FOUR, f - TWO, lax.rem(f, TWO), (ONE,))))
 
         scatter.tick(j, PLAN)
 
-        @pl.when(in1)
-        def _():
-            f = j - S1
-            slot = lax.rem(f, TWO)
-            layer1(f, slot)
-            go(put_ob(ONE, f, slot))
-            put_tl(f, slot).start()
-
-        when(in2, lambda: down_grad(j - S2, r1, ZERO))
-        when(in6, lambda: down_grad(j - S6, r2, THREE))
+        @pl.when(j < S3)
+        def _():
+            @pl.when(in1)
+            def _():
+                f = j - S1
+                slot = lax.rem(f, TWO)
+                layer1(f, slot)
+                go(put_ob(ONE, f, slot))
+                put_tl(f, slot).start()
+
+            when(in2, lambda: down_grad(j - S2, r1, ZERO))
 
         @pl.when(in3 | in9)
         def _():
@@ -961,50 +966,54 @@
                 norm_back(THREE)
                 when(in9, lambda: put_dx(THREE).start())
 
-        @pl.when(in5)
-        def _():
-            s = j - S5
-            half, t = s // FOUR, lax.rem(s, FOUR)
-            when(t == ZERO, lambda: down_rows(half))
-            v = dot(dh[rows(t), :], am[: FF // TWO, :], NT).astype(bf)
-            for c in range(C // TWO):
-                r1[C // TWO * half + c, rows(t), :] = v[:, L * c : L * c + L]
-            when(s == SEVEN, lambda: load_am(a0).start())
-
-        @pl.when(in7)
-        def _():
-            i = j - S7
-            before = i - ONE
-            slot = lax.rem(i + ONE, TWO)
-            tiles = lambda: [r2[TWO * before], r2[TWO * before + ONE]]
-
-            @pl.when(i == ZERO)
-            def _():
-                for e in (ZERO, ONE):
-                    done(load_gl(ZERO, e))
-                    for t in range(FOUR):
-                        silu_back(ZERO, e, t)
-                    go(load_gl(ONE, e))
-
-            @pl.when((i > ZERO) & (i < N_F))
-            def _():
-                for e in (ZERO, ONE):
-                    done(load_gl(i, e))
-                    for t in (ZERO, ONE):
-                        gate_up_grad(slot, tiles(), (TWO * e + t, TWO * e + t + ONE), (ZERO,))
-                        silu_back(i, e, TWO * t)
-                        silu_back(i, e, TWO * t + ONE)
-                    when(i + ONE < N_F, lambda: go(load_gl(i + ONE, e)))
-
-            when(i == N_F, lambda: gate_up_grad(slot, tiles(), (ZERO, FOUR), (ZERO,)))
-            when(i > ZERO, lambda: go(put_ob(FOUR, before, slot, (ZERO,))))
-
-        @pl.when(in8)
-        def _():
-            f = j - S8
-            slot = lax.rem(f, TWO)
-            gate_up_grad(slot, [r1[TWO * f], r1[TWO * f + ONE]], (ZERO, FOUR), (ONE,))
-            go(put_ob(FOUR, f, slot, (ONE,)))
+        @pl.when((j >= S6) & (j < S9))
+        def _():
+            when(in6, lambda: down_grad(j - S6, r2, THREE))
+
+            @pl.when(in5)
+            def _():
+                s = j - S5
+                half, t = s // FOUR, lax.rem(s, FOUR)
+                when(t == ZERO, lambda: down_rows(half))
+                v = dot(dh[rows(t), :], am[: FF // TWO, :], NT).astype(bf)
+                for c in range(C // TWO):
+                    r1[C // TWO * half + c, rows(t), :] = v[:, L * c : L * c + L]
+                when(s == SEVEN, lambda: load_am(a0).start())
+
+            @pl.when(in7)
+            def _():
+                i = j - S7
+                before = i - ONE
+                slot = lax.rem(i + ONE, TWO)
+                tiles = lambda: [r2[TWO * before], r2[TWO * before + ONE]]
+
+                @pl.when(i == ZERO)
+                def _():
+                    for e in (ZERO, ONE):
+                        done(load_gl(ZERO, e))
+                        for t in range(FOUR):
+                            silu_back(ZERO, e, t)
+                        go(load_gl(ONE, e))
+
+                @pl.when((i > ZERO) & (i < N_F))
+                def _():
+                    for e in (ZERO, ONE):
+                        done(load_gl(i, e))
+                        for t in (ZERO, ONE):
+                            gate_up_grad(slot, tiles(), (TWO * e + t, TWO * e + t + ONE), (ZERO,))
+                            silu_back(i, e, TWO * t)
+                            silu_back(i, e, TWO * t + ONE)
+                        when(i + ONE < N_F, lambda: go(load_gl(i + ONE, e)))
+
+                when(i == N_F, lambda: gate_up_grad(slot, tiles(), (ZERO, FOUR), (ZERO,)))
+                when(i > ZERO, lambda: go(put_ob(FOUR, before, slot, (ZERO,))))
+
+            @pl.when(in8)
+            def _():
+                f = j - S8
+                slot = lax.rem(f, TWO)
+                gate_up_grad(slot, [r1[TWO * f], r1[TWO * f + ONE]], (ZERO, FOUR), (ONE,))
+                go(put_ob(FOUR, f, slot, (ONE,)))
 
         return ZERO
 

time: 401 us -> 397 us (0.990)
    pallas_call x1, Pallas kernels: 276 us -> 272 us  [backward(): pl.pallas_call(backward_kernel, in_specs=[HBM] * TWELVE, out_specs=[HBM]...]
where the time goes in v5:
time: 397 us; the launch traced here: 396 us
  Pallas kernels  384 us (97%)
  local copies, waits for them, and re-layouts  10.7 us (3%)
    pallas_call x1, Pallas kernels, backward(): pl.pallas_call(backward_kernel, in_specs=[HBM] * TWELVE, out_specs=[HBM]...  272 us
    pallas_call x1, Pallas kernels, forward(): pl.pallas_call(forward_kernel, in_specs=[HBM, HBM, VMEM, VMEM, VMEM], out...  112 us

profile of v5, /device:TPU:0, one launch (start us, length us, event | category | flops | bytes accessed | tf_op | source)
XLA Modules:
  0.0 396.1 jit_solution(2113170228069474467)
XLA Ops:
  0.6 0.8 slice.16
  1.5 1.0 slice.15
  2.5 0.1 reshape.32
  2.7 0.7 pad_maximum_fusion.1
  3.4 112.3 %forward.1 = (bf16[2,22,4,4,4,16,128]{6,5,4,3,2,1,0:T(8,128)(2,1)}, bf16[2,11,4,4,4,16,128]{6,5,4,3,2,1,0:T(8,128)(2,1)}, bf16[2,22,4,4,4,16,128]{6,5,4,3,2,1,0:...) custom-call(bf16[2048,1024]{1,0:T(8,128)(2,1)} %bitcast.14, ...), custom_call_target="tpu_custom_call" | custom-call | tf_op jit(solution)/shard_map/forward/pallas_call | solution.py:378
  115.7 271.7 %backward.1 = (bf16[2048,1024]{1,0:T(8,128)(2,1)}, bf16[2,16,2816]{2,1,0:T(8,128)(2,1)}, bf16[2,16,2816]{2,1,0:T(8,128)(2,1)}, bf16[2,16,2816]{2,1,0:T(8,128)(2,...) custom-call(bf16[2048,1024]{1,0:T(8,128)(2,1)} %bitcast.15, ...), custom_call_target="tpu_custom_call" | custom-call | tf_op jit(solution)/shard_map/backward/pallas_call | solution.py:1032
  387.4 0.0 copy-start.1
  387.4 0.0 copy-start
  387.4 0.9 slice.19
  388.3 0.9 fusion
  389.3 0.9 copy.17
  390.2 4.6 %copy.23 = bf16[1,2048,1024]{2,1,0:T(8,128)(2,1)} copy(bf16[1,2048,1024]{2,1,0:T(8,128)(2,1)} %bitcast.19) | data formatting | bytes 8388608
  394.8 0.0 copy-done.1
  394.8 0.7 copy.24
  395.5 0.0 copy-done
  395.5 0.7 copy.25
  (7 shorter events, 0.2 us)
Async XLA Ops:
  387.4 7.4 %copy-start.1 = (bf16[2,16,2816]{2,1,0:T(8,128)(2,1)S(1)}, bf16[2,16,2816]{2,1,0:T(8,128)(2,1)}, u32[]{:S(2)}) copy-start(bf16[2,16,2816]{2,1,0:T(8,128)(2,1)} %get-tuple-element.47) | copy-start | bytes 540676
  387.4 8.1 %copy-start = (bf16[2,16,2816]{2,1,0:T(8,128)(2,1)S(1)}, bf16[2,16,2816]{2,1,0:T(8,128)(2,1)}, u32[]{:S(2)}) copy-start(bf16[2,16,2816]{2,1,0:T(8,128)(2,1)} %get-tuple-element.48) | copy-start | bytes 540676

commit v6 on v5

--- a/solution.py
+++ b/solution.py
@@ -156,8 +156,14 @@
 
 
 def down_block(tiles):
-    last = [wide([tiles[ROWS + TWO * g + e][FOUR * c : FOUR * c + FOUR] for c in range(FOUR) for e in (ZERO, ONE)]) for g in range(THREE)]
-    return jnp.concatenate([wide(tiles[:EIGHT]), wide(tiles[EIGHT:ROWS]), *last], axis=ZERO)
+    last = []
+    for q in range(EIGHT):
+        tile, row = ROWS + TWELVE * q // ROWS, TWELVE * q % ROWS
+        parts = [tiles[tile][row : min(row + TWELVE, ROWS)]]
+        if row + TWELVE > ROWS:
+            parts.append(tiles[tile + ONE][: row - FOUR])
+        last.append(jnp.concatenate(parts, axis=ZERO))
+    return jnp.concatenate([wide(tiles[:EIGHT]), wide(tiles[EIGHT:ROWS]), wide(last)], axis=ZERO)
 
 
 def plan_forward():
@@ -762,14 +768,11 @@
                 for e in (ZERO, ONE):
                     stg[TWO * c + e, x, y, z] = v[44 * z : 44 * z + ROWS, lanes[e]]
                     stg[EIGHT + TWO * c + e, x, y, z] = v[44 * z + ROWS : 44 * z + 32, lanes[e]]
-            for k in range(FOUR):
-
-                @pl.when(c == k)
-                def _():
-                    for z in range(FOUR):
-                        for n in range(THREE):
-                            for e in (ZERO, ONE):
-                                stg[ROWS + TWO * n + e, x, y, z, FOUR * k : FOUR * k + FOUR] = v[44 * z + 32 + FOUR * n : 44 * z + 36 + FOUR * n, lanes[e]]
+            for z in range(FOUR):
+                one, two = (v[44 * z + 32 : 44 * z + 44, lanes[e]] for e in (ZERO, ONE))
+                for k, part in enumerate((one[:EIGHT], jnp.concatenate([one[EIGHT:], two[:FOUR]], axis=ZERO), two[FOUR:])):
+                    n = THREE * c + k
+                    stg[ROWS + n // TWO, x, y, z, pl.ds(pl.multiple_of(EIGHT * lax.rem(n, TWO), EIGHT), EIGHT)] = part
 
             return ZERO
 
@@ -1048,12 +1051,12 @@
 
 def pack_down(t):
     first = t[:, :32].reshape(-ONE, TWO, ROWS, EIGHT, L).transpose(ZERO, ONE, THREE, TWO, FOUR).reshape(-ONE, ROWS, ROWS, L)
-    last = t[:, 32:].reshape(-ONE, THREE, FOUR, FOUR, TWO, L).transpose(ZERO, ONE, FOUR, THREE, TWO, FIVE).reshape(-ONE, SIX, ROWS, L)
+    last = t[:, 32:].reshape(-ONE, TWELVE, EIGHT, L).transpose(ZERO, TWO, ONE, THREE).reshape(-ONE, SIX, ROWS, L)
     return jnp.concatenate([first, last], axis=ONE).reshape(-ONE, TWO, C // TWO, ROWS, L)
 
 
 def unpack_down(t):
-    last = t[:, :, TWO * D :].reshape(-ONE, FOUR, FOUR, THREE, F).transpose(ZERO, THREE, TWO, ONE, FOUR).reshape(-ONE, TWELVE, D)
+    last = t[:, :, TWO * D :].reshape(-ONE, ROWS, SIX, L).transpose(ZERO, TWO, ONE, THREE).reshape(-ONE, EIGHT, TWELVE, L).transpose(ZERO, TWO, ONE, THREE).reshape(-ONE, TWELVE, D)
     return jnp.concatenate([t[:, :, :D], t[:, :, D : TWO * D], last], axis=ONE)
 
 

time: 397 us -> 395 us (level)
  no operation moved by 1% of the time
where the time goes in v6:
time: 395 us; the launch traced here: 394 us
  Pallas kernels  382 us (97%)
  local copies, waits for them, and re-layouts  10.7 us (3%)
    pallas_call x1, Pallas kernels, backward(): pl.pallas_call(backward_kernel, in_specs=[HBM] * TWELVE, out_specs=[HBM]...  270 us
    pallas_call x1, Pallas kernels, forward(): pl.pallas_call(forward_kernel, in_specs=[HBM, HBM, VMEM, VMEM, VMEM], out...  112 us

profile of v6, /device:TPU:0, one launch (start us, length us, event | category | flops | bytes accessed | tf_op | source)
XLA Modules:
  0.0 394.5 jit_solution(5072294043313838079)
XLA Ops:
  0.6 0.8 copy_bitcast_fusion
  1.5 1.0 slice.15
  2.5 0.1 reshape.35
  2.6 0.7 pad_maximum_fusion.1
  3.3 112.0 %forward.1 = (bf16[2,22,4,4,4,16,128]{6,5,4,3,2,1,0:T(8,128)(2,1)}, bf16[2,11,4,4,4,16,128]{6,5,4,3,2,1,0:T(8,128)(2,1)}, bf16[2,22,4,4,4,16,128]{6,5,4,3,2,1,0:...) custom-call(bf16[2048,1024]{1,0:T(8,128)(2,1)} %bitcast.23, ...), custom_call_target="tpu_custom_call" | custom-call | tf_op jit(solution)/shard_map/forward/pallas_call | solution.py:384
  115.4 270.3 %backward.1 = (bf16[2048,1024]{1,0:T(8,128)(2,1)}, bf16[2,16,2816]{2,1,0:T(8,128)(2,1)}, bf16[2,16,2816]{2,1,0:T(8,128)(2,1)}, bf16[2,16,2816]{2,1,0:T(8,128)(2,...) custom-call(bf16[2048,1024]{1,0:T(8,128)(2,1)} %bitcast.24, ...), custom_call_target="tpu_custom_call" | custom-call | tf_op jit(solution)/shard_map/backward/pallas_call | solution.py:1035
  385.6 0.0 copy-start.1
  385.6 0.0 copy-start
  385.7 0.9 slice.19
  386.5 0.9 fusion
  387.4 0.1 reshape.41
  387.5 0.1 copy.15
  387.6 0.1 reshape.44
  387.6 0.9 copy.18
  388.5 4.6 %copy.26 = bf16[1,2048,1024]{2,1,0:T(8,128)(2,1)} copy(bf16[1,2048,1024]{2,1,0:T(8,128)(2,1)} %bitcast.28) | data formatting | bytes 8388608
  393.1 0.0 copy-done.1
  393.1 0.7 copy.27
  393.8 0.0 copy-done
  393.8 0.7 copy.28
  (4 shorter events, 0.1 us)
Async XLA Ops:
  385.6 7.5 %copy-start.1 = (bf16[2,16,2816]{2,1,0:T(8,128)(2,1)S(1)}, bf16[2,16,2816]{2,1,0:T(8,128)(2,1)}, u32[]{:S(2)}) copy-start(bf16[2,16,2816]{2,1,0:T(8,128)(2,1)} %get-tuple-element.47) | copy-start | bytes 540676
  385.6 8.2 %copy-start = (bf16[2,16,2816]{2,1,0:T(8,128)(2,1)S(1)}, bf16[2,16,2816]{2,1,0:T(8,128)(2,1)}, u32[]{:S(2)}) copy-start(bf16[2,16,2816]{2,1,0:T(8,128)(2,1)} %get-tuple-element.48) | copy-start | bytes 540676
